TPU v7x, 256 devices: a whole 4x4x8 slice. The times are simulated.
256 devices in a mesh: grp: 16 (over y, z_hi, core), dp: 16 (over z_lo, x).
Axes of the slice: x: 4, y: 4, z: 8 (z_hi: 2, z_lo: 4; z = z_hi * 4 + z_lo), core: 2. Of those that a mesh axis runs over, the one named last changes fastest.
Arguments:
- tokens: bfloat16 [16, 2048, 2048], P('grp', 'dp'), may hold values from -6 to 6
- hidden_grad: bfloat16 [16, 2048, 6144], P('grp', 'dp'), may hold values from -6 to 6
- w_gate: bfloat16 [16, 2048, 6144], P('grp', None, 'dp'), may hold values from -6 to 6
- w_up: bfloat16 [16, 2048, 6144], P('grp', None, 'dp'), may hold values from -6 to 6
Outputs:
- mixed_gate: bfloat16 [16, 2048, 6144], P('grp', None, 'dp')
- mixed_up: bfloat16 [16, 2048, 6144], P('grp', None, 'dp')
All inputs are finite; a program needn't handle non-finite values.
Results may differ from a plain program's by a relative error of at most 0.0052.
Values may be sent and summed in bfloat16 or wider, within the bound.
No kernel may reach another device: no remote copies, remote signals or barrier semaphores. Data moves between devices by JAX's collectives and lax.ppermute only.
A program may use at most 256 MiB of HBM per device.

v0:
```python
import jax
import jax.numpy as jnp
from jax import lax
from jax.sharding import PartitionSpec as P


def from_behind(x, axis, by):
    size = lax.axis_size(axis)
    return lax.ppermute(x, axis, [(i, (i + by) % size) for i in range(size)])


def gating(rows, cotangent, gate_weight, up_weight):
    scale = rows.shape[1] ** (-0.5)
    gate = jnp.dot(rows, gate_weight, preferred_element_type=jnp.float32) * scale
    up = jnp.dot(rows, up_weight, preferred_element_type=jnp.float32) * scale
    sigma = jax.nn.sigmoid(gate)
    upstream = cotangent.astype(jnp.float32)
    gate_rows = upstream * up * sigma * (1.0 + gate * (1.0 - sigma))
    up_rows = upstream * gate * sigma
    return jnp.stack([gate_rows, up_rows]).astype(jnp.bfloat16)


def local(tokens, hidden_grad, w_gate, w_up):
    local_rows = tokens[0]
    gate_weight = w_gate[0]
    up_weight = w_up[0]
    width = local_rows.shape[1]
    scale = width ** (-0.5)
    unit_cotangent = lax.all_to_all(hidden_grad[0], "dp", split_axis=1, concat_axis=0, tiled=True)
    gathered = lax.all_gather(local_rows, "dp", axis=0, tiled=True)
    unit_rows = gating(gathered, unit_cotangent, gate_weight, up_weight)
    gradient = jnp.einsum("rd,krf->kdf", gathered, unit_rows, preferred_element_type=jnp.float32)
    weights = jnp.concatenate([w_gate, w_up], axis=0).astype(jnp.float32)
    stepped = (weights - 0.5 * (gradient * scale)).astype(jnp.bfloat16)
    left_side = from_behind(stepped, "grp", 1)
    right_side = from_behind(stepped, "grp", -1)
    mixed = 0.5 * stepped.astype(jnp.float32) + 0.25 * (
        left_side.astype(jnp.float32) + right_side.astype(jnp.float32)
    )
    mixed = mixed.astype(jnp.bfloat16)
    return (mixed[0:1], mixed[1:2])


def solution(mesh):
    in_specs = (
        P("grp", "dp", None),
        P("grp", "dp", None),
        P("grp", None, "dp"),
        P("grp", None, "dp"),
    )
    out_specs = (P("grp", None, "dp"), P("grp", None, "dp"))
    return jax.shard_map(local, mesh=mesh, in_specs=in_specs, out_specs=out_specs, check_vma=False)
```

profile of v0, /device:TPU:38, one launch (start us, length us, event | category | flops | bytes accessed | tf_op | source)
XLA Modules:
  0.0 321.6 jit_solution(314343980765271977)
XLA Ops:
  7.2 0.0 all-gather.3.cloned.1.call-start
  7.2 0.7 all-gather.3.cloned.1.call-update
  7.9 1.7 copy.13
  9.6 0.0 copy-start
  9.6 1.5 copy.8
  11.1 0.0 copy-start.1
  11.1 8.5 %all-to-all-start = ((bf16[128,16,384]{2,0,1:T(8,128)(2,1)}), bf16[128,16,384]{2,0,1:T(8,128)(2,1)}, u32[]{:S(2)}, u32[]{:S(2)}) async-start(bf16[128,16,384]{2,0,1:T(8,128)(2,1)} %copy.8), calls=%async_computation | async-start | bytes 3145728 | tf_op jit(solution)/shard_map/all_to_all | solution.py:29
  19.7 0.0 copy-done
  19.7 1.6 copy.6
  21.3 0.0 copy-done.1
  21.3 1.6 copy.7
  22.9 109.3 %all-to-all-done = bf16[128,16,384]{2,0,1:T(8,128)(2,1)} async-done(((bf16[128,16,384]{2,0,1:T(8,128)(2,1)}), bf16[128,16,384]{2,0,1:T(8,128)(2,1)}, u32[]{:S(2)}, u32[]{:S(2)}) %all-to-all-start) | async-done | bytes 1572896 | tf_op jit(solution)/shard_map/all_to_all | solution.py:29
  132.3 8.1 %all-gather.3.cloned.1.call-done = bf16[1,2048,2048]{2,1,0:T(8,128)(2,1)} async-done(((bf16[1,128,2048]{2,1,0:T(8,128)(2,1)}), bf16[1,2048,2048]{2,1,0:T(8,128)(2,1)}) %all-gather.3.cloned.1.call-update) | async-done | bytes 8388624 | tf_op jit(solution)/shard_map/all_gather | solution.py:30
  140.4 0.0 copy-start.4
  140.4 9.3 %fusion.16 = (bf16[2048,384]{1,0:T(8,128)(2,1)S(1)}, f32[2048,384]{1,0:T(8,128)S(1)}) fusion(bf16[128,16,384]{2,0,1:T(8,128)(2,1)} %all-to-all-done, bf16[1,2048,384]{2,1,0:T(8,128)(2,1)S(1)} %copy-done, bf16[1,2048,2048]{2,1,0:T(8,128)(2,1)} %all-gather.3.cloned.1.call-done), kind=kOutput, calls=%fused_computation.18 | convolution fusion | flops 3227516928 | bytes 16252928 | tf_op jit(solution)/shard_map/dot_general | solution.py:14
  149.7 0.0 copy-done.4
  149.7 0.0 copy-start.2
  149.7 0.0 copy-start.3
  149.7 6.7 %fusion.22 = bf16[1,2048,384]{2,1,0:T(8,128)(2,1)S(1)} fusion(f32[2048,384]{1,0:T(8,128)S(1)} %get-tuple-element.7, bf16[1,2048,2048]{2,1,0:T(8,128)(2,1)S(1)} %copy-done.4, bf16[128,16,384]{2,0,1:T(8,128)(2,1)} %all-to-all-done, bf16[1,2048,384]{2,1,0:T(8,128)(2,1)S(1)} %copy-done.1), kind=kOutput, calls=%fused_computation.21 | convolution fusion | flops 3230662656 | bytes 16252928 | tf_op jit(solution)/shard_map/dot_general | solution.py:15
  156.4 0.0 copy-done.2
  156.4 0.0 copy-done.3
  156.4 8.8 %fusion.6 = bf16[2,2048,384]{1,2,0:T(8,128)(2,1)S(1)} fusion(bf16[1,2048,2048]{2,1,0:T(8,128)(2,1)S(1)} %copy-done.4, bf16[1,2048,384]{1,2,0:T(8,128)(2,1)S(1)} %copy-done.3, bf16[1,2048,384]{1,2,0:T(8,128)(2,1)S(1)} %copy-done.2, bf16[1,2048,384]{2,1,0:T(8,128)(2,1)S(1)} %bitcast.55, bf16[1,2048,384]{2,1,0:T(8,128)(2,1)S(1)} %fusion.22), kind=kOutput, calls=%fused_computation.7 | convolution fusion | flops 6451888128 | bytes 17825792 | tf_op jit(solution)/shard_map/rd,krf->kdf/dot_general | solution.py:32
  165.2 0.1 collective-permute-start
  165.3 7.8 %collective-permute-start.1 = (bf16[2,2048,384]{1,2,0:T(8,128)(2,1)S(1)}, bf16[2,2048,384]{1,2,0:T(8,128)(2,1)S(1)}, u32[]{:S(2)}, u32[]{:S(2)}) collective-permute-start(bf16[2,2048,384]{1,2,0:T(8,128)(2,1)S(1)} %fusion.6), channel_id=1, source_target_pairs={{0,240},{16,0},{32,16},{48,32},{64,48},{80,64},{96,80},{112,96},{1... | collective-permute-start | bytes 9437192 | tf_op jit(solution)/shard_map/ppermute | solution.py:9
  173.1 135.6 %collective-permute-done = bf16[2,2048,384]{1,2,0:T(8,128)(2,1)S(1)} collective-permute-done((bf16[2,2048,384]{1,2,0:T(8,128)(2,1)S(1)}, bf16[2,2048,384]{1,2,0:T(8,128)(2,1)S(1)}, u32[]{:S(2)}, u32[]{:S(2)}) %collective-permute-start) | collective-permute-done | bytes 3145760 | tf_op jit(solution)/shard_map/ppermute | solution.py:9
  308.7 0.0 collective-permute-done.1
  308.7 2.5 add_convert_fusion
  311.2 0.4 fusion.28
  311.6 1.6 copy.10
  313.2 1.6 copy.11
Async XLA Ops:
  7.2 133.2 %all-gather.3.cloned.1.call-start = ((), (), s32[]{:S(2)}) async-start(), calls=%async_computation.1 | async-start | bytes 8912896 | tf_op jit(solution)/shard_map/all_gather | solution.py:30
  9.6 10.1 %copy-start = (bf16[1,2048,384]{2,1,0:T(8,128)(2,1)S(1)}, bf16[1,2048,384]{2,1,0:T(8,128)(2,1)}, u32[]{:S(2)}) copy-start(bf16[1,2048,384]{2,1,0:T(8,128)(2,1)} %param.6) | copy-start | bytes 4718596
  11.1 10.2 %copy-start.1 = (bf16[1,2048,384]{2,1,0:T(8,128)(2,1)S(1)}, bf16[1,2048,384]{2,1,0:T(8,128)(2,1)}, u32[]{:S(2)}) copy-start(bf16[1,2048,384]{2,1,0:T(8,128)(2,1)} %param.7) | copy-start | bytes 4718596
  11.1 121.1 %all-to-all-start = ((bf16[128,16,384]{2,0,1:T(8,128)(2,1)}), bf16[128,16,384]{2,0,1:T(8,128)(2,1)}, u32[]{:S(2)}, u32[]{:S(2)}) async-start(bf16[128,16,384]{2,0,1:T(8,128)(2,1)} %copy.8), calls=%async_computation | async-start | bytes 3145728 | tf_op jit(solution)/shard_map/all_to_all | solution.py:29
  140.4 9.3 %copy-start.4 = (bf16[1,2048,2048]{2,1,0:T(8,128)(2,1)S(1)}, bf16[1,2048,2048]{2,1,0:T(8,128)(2,1)}, u32[]{:S(2)}) copy-start(bf16[1,2048,2048]{2,1,0:T(8,128)(2,1)} %all-gather.3.cloned.1.call-done) | copy-start | bytes 25165828
  149.7 6.7 %copy-start.2 = (bf16[1,2048,384]{1,2,0:T(8,128)(2,1)S(1)}, bf16[1,2048,384]{1,2,0:T(8,128)(2,1)}, u32[]{:S(2)}) copy-start(bf16[1,2048,384]{1,2,0:T(8,128)(2,1)} %copy.6) | copy-start | bytes 4718596
  149.7 6.7 %copy-start.3 = (bf16[1,2048,384]{1,2,0:T(8,128)(2,1)S(1)}, bf16[1,2048,384]{1,2,0:T(8,128)(2,1)}, u32[]{:S(2)}) copy-start(bf16[1,2048,384]{1,2,0:T(8,128)(2,1)} %copy.7) | copy-start | bytes 4718596
  165.2 143.5 %collective-permute-start = (bf16[2,2048,384]{1,2,0:T(8,128)(2,1)S(1)}, bf16[2,2048,384]{1,2,0:T(8,128)(2,1)S(1)}, u32[]{:S(2)}, u32[]{:S(2)}) collective-permute-start(bf16[2,2048,384]{1,2,0:T(8,128)(2,1)S(1)} %fusion.6), channel_id=1, source_target_pairs={{0,16},{16,32},{32,48},{48,64},{64,80},{80,96},{96,112},{112,128},... | collective-permute-start | bytes 9437192 | tf_op jit(solution)/shard_map/ppermute | solution.py:9
  165.3 143.4 %collective-permute-start.1 = (bf16[2,2048,384]{1,2,0:T(8,128)(2,1)S(1)}, bf16[2,2048,384]{1,2,0:T(8,128)(2,1)S(1)}, u32[]{:S(2)}, u32[]{:S(2)}) collective-permute-start(bf16[2,2048,384]{1,2,0:T(8,128)(2,1)S(1)} %fusion.6), channel_id=1, source_target_pairs={{0,240},{16,0},{32,16},{48,32},{64,48},{80,64},{96,80},{112,96},{1... | collective-permute-start | bytes 9437192 | tf_op jit(solution)/shard_map/ppermute | solution.py:9
Sparse Core Ops, SparseCore 0:
  9.8 130.5 all-gather.2
where the time goes:
time: 322 us
  waiting for transfers between devices  254 us (79%)
  matrix products  24.8 us (8%)
  starting transfers between devices  16.4 us (5%)
  between operations  14.1 us (4%)
  local copies, waits for them, and re-layouts  10 us (3%)
    ppermute x2, waiting for transfers between devices, from_behind(): return lax.ppermute(x, axis, [(i, (i + by) % size) for i in range(size)])  136 us
    all_to_all x1, waiting for transfers between devices, local(): lax.all_to_all(hidden_grad[0], 'dp', split_axis=1, concat_axis=0, tiled=T...  109 us
    dot_general x1, matrix products, gating(): jnp.dot(rows, gate_weight, preferred_element_type=jnp.float32) * scale  9.29 us
    dot_general x1, matrix products, local(): jnp.einsum('rd,krf->kdf', gathered, unit_rows, preferred_element_type=jnp...  8.8 us
    all_to_all x1, starting transfers between devices, local(): lax.all_to_all(hidden_grad[0], 'dp', split_axis=1, concat_axis=0, tiled=T...  8.53 us
    unnamed x15, local copies, waits for them, and re-layouts  8.12 us
    all_gather x1, waiting for transfers between devices, local(): gathered = lax.all_gather(local_rows, 'dp', axis=0, tiled=True)  8.11 us
    ppermute x2, starting transfers between devices, from_behind(): return lax.ppermute(x, axis, [(i, (i + by) % size) for i in range(size)])  7.83 us
  transfers between devices with their start and end apart: 4, of which 3 were waited for; matrix products, arithmetic and copies ran while one was open for 2% of the time, Pallas kernels for 0%

commit v1 on v0

v1 whole, which is shorter than its diff:
```python
import functools

import jax
import jax.numpy as jnp
from jax import lax
from jax.experimental import pallas as pl
from jax.experimental.pallas import tpu as pltpu
from jax.sharding import PartitionSpec as P


NZ = 4
NX = 4
DX = (0, 1, -1, 2)
CHUNKS = 3
VMEM = pl.BlockSpec(memory_space=pltpu.VMEM)
SMEM = pl.BlockSpec(memory_space=pltpu.SMEM)
ANY = pl.BlockSpec(memory_space=pl.ANY)
HBM = pl.BlockSpec(memory_space=pltpu.HBM)
MIB = 1024 * 1024


def params(mib):
    return pltpu.CompilerParams(vmem_limit_bytes=mib * MIB)


def device_pairs(grp, move):
    out = []
    for g in range(grp):
        for z in range(NZ):
            for x in range(NX):
                to = move(g, z, x)
                if to is not None:
                    h, u, v = to
                    out.append(((g * NZ + z) * NX + x, ((h % grp) * NZ + u % NZ) * NX + v % NX))
    return out


def split_body(hg, *refs):
    out = refs[-1]
    units = out.shape[2]
    for i in range(out.shape[0]):
        out[i] = hg[:, i * units:(i + 1) * units]


def split_units(hg, parts, *deps):
    rows, width = hg.shape
    return pl.pallas_call(
        split_body,
        out_shape=jax.ShapeDtypeStruct((parts, rows, width // parts), hg.dtype),
        in_specs=[VMEM] + [HBM] * len(deps),
        out_specs=VMEM,
        compiler_params=params(8),
        name="split",
    )(hg, *deps)


def pack_body(g, u, out):
    uw = g.shape[1]
    out[0, :, :uw] = g[...]
    out[0, :, uw:] = u[...]


def pack_weights(g, u):
    width, units = g.shape
    uw = units // CHUNKS
    read = pl.BlockSpec((width, uw), lambda c: (0, c))
    return pl.pallas_call(
        pack_body,
        grid=(CHUNKS,),
        out_shape=jax.ShapeDtypeStruct((CHUNKS, width, 2 * uw), g.dtype),
        in_specs=[read, read],
        out_specs=pl.BlockSpec((1, width, 2 * uw), lambda c: (c, 0, 0)),
        compiler_params=params(10),
        name="pack",
    )(g, u)


def cat_body(count, *refs):
    xs, out, sems = refs[:count], refs[-2], refs[-1]
    copies, at = [], 0
    for i, v in enumerate(xs):
        copies.append(pltpu.make_async_copy(v, out.at[pl.ds(at, v.shape[0])], sems.at[i]))
        at += v.shape[0]
    for c in copies:
        c.start()
    for c in copies:
        c.wait()


def cat(xs, *deps):
    n = sum(v.shape[0] for v in xs)
    return pl.pallas_call(
        functools.partial(cat_body, len(xs)),
        out_shape=jax.ShapeDtypeStruct((n,) + xs[0].shape[1:], xs[0].dtype),
        in_specs=[HBM] * (len(xs) + len(deps)),
        out_specs=HBM,
        scratch_shapes=[pltpu.SemaphoreType.DMA((len(xs),))],
        compiler_params=params(4),
        name="cat",
    )(*xs, *deps)


def step_body(which, count, meta, hg, w, *refs):
    xs = refs[:count]
    rest = refs[count:]
    other = rest[0] if which == 1 else None
    out, x, rows, sems = rest[-4:]
    uw = w.shape[2] // 2
    blk = hg.shape[1]
    part = 512
    scale = w.shape[1] ** (-0.5)

    @pl.when(meta[0] == which)
    def _():
        at = 0
        for v in xs:
            pltpu.make_async_copy(v, x.at[pl.ds(at, v.shape[0])], sems.at[at // part]).start()
            at += v.shape[0]

        def products(i, carry):
            at = pl.multiple_of(i * part, part)
            here = x.at[pl.ds(at, part)]
            pltpu.make_async_copy(here, here, sems.at[i]).wait()
            gu = jnp.dot(x[pl.ds(at, part), :], w[0], preferred_element_type=jnp.float32) * scale
            for j in range(part // blk):
                gate = gu[j * blk:(j + 1) * blk, :uw]
                up = gu[j * blk:(j + 1) * blk, uw:]
                upstream = hg[meta[1 + i * (part // blk) + j]].astype(jnp.float32)
                sigma = jax.nn.sigmoid(gate)
                g = upstream * up * sigma * (1.0 + gate * (1.0 - sigma))
                u = upstream * gate * sigma
                to = pl.ds(pl.multiple_of(at + j * blk, blk), blk)
                rows[to, :uw] = g.astype(jnp.bfloat16)
                rows[to, uw:] = u.astype(jnp.bfloat16)
            return carry

        lax.fori_loop(0, x.shape[0] // part, products, 0)

        def band(i, carry):
            at = pl.multiple_of(i * part, part)
            grad = lax.dot_general(x[:, pl.ds(at, part)], rows[...], (((0,), (0,)), ((), ())), preferred_element_type=jnp.float32)
            old = w[0, pl.ds(at, part), :].astype(jnp.float32)
            out[pl.ds(at, part), :] = (old - 0.5 * (grad * scale)).astype(jnp.bfloat16)
            return carry

        lax.fori_loop(0, w.shape[1] // part, band, 0)

    if other is not None:
        @pl.when(meta[0] != which)
        def _():
            pltpu.sync_copy(other, out)


def step_chunk(which, c, meta, hg, w, xs, *extra):
    width = w.shape[1]
    n = sum(v.shape[0] for v in xs)
    both = w.shape[2]
    return pl.pallas_call(
        functools.partial(step_body, which, len(xs)),
        grid=(1,),
        out_shape=jax.ShapeDtypeStruct((width, both), jnp.bfloat16),
        in_specs=[
            SMEM,
            pl.BlockSpec(hg.shape[:2] + (both // 2,), lambda i: (0, 0, c)),
            pl.BlockSpec((1, width, both), lambda i: (c, 0, 0)),
        ]
        + [HBM] * (len(xs) + len(extra)),
        out_specs=pl.BlockSpec((width, both), lambda i: (0, 0)),
        scratch_shapes=[
            pltpu.VMEM((n, width), jnp.bfloat16),
            pltpu.VMEM((n, both), jnp.bfloat16),
            pltpu.SemaphoreType.DMA((n // 512,)),
        ],
        compiler_params=params(32),
        cost_estimate=pl.CostEstimate(flops=4 * n * width * both, bytes_accessed=n * width * 2, transcendentals=n * 128),
        name="step",
    )(meta, hg, w, *xs, *extra)


def mix_body(meta, own, near, far_a, far_b, *refs):
    og, ou = refs[-2:]
    uw = og.shape[1]
    f = jnp.float32

    def store(far):
        m = 0.5 * own[...].astype(f) + 0.25 * (near[...].astype(f) + far[...].astype(f))
        m = m.astype(jnp.bfloat16)
        og[...] = m[:, :uw]
        ou[...] = m[:, uw:]

    @pl.when(meta[0] == 0)
    def _():
        store(far_b)

    @pl.when(meta[0] == 1)
    def _():
        store(far_a)


def mix_chunk(c, meta, own, near, far_a, far_b, done):
    width, both = own.shape
    uw = both // 2
    band = 512
    read = pl.BlockSpec((band, both), lambda i: (i, 0))
    write = pl.BlockSpec((band, uw), lambda i: (i, c))
    extra = [] if done is None else list(done)
    return pl.pallas_call(
        mix_body,
        grid=(width // band,),
        out_shape=(jax.ShapeDtypeStruct((width, CHUNKS * uw), jnp.bfloat16),) * 2,
        in_specs=[SMEM] + [read] * 4 + [ANY] * len(extra),
        out_specs=(write, write),
        input_output_aliases={} if done is None else {5: 0, 6: 1},
        compiler_params=params(10),
        name="mix",
    )(meta, own, near, far_a, far_b, *extra)


def local(tokens, hidden_grad, w_gate, w_up):
    axes = ("grp", "dp")
    groups = lax.axis_size("grp")
    own = tokens[0]
    dp = lax.axis_index("dp")
    core = lax.axis_index("grp") % 2
    z, x = dp // NX, dp % NX

    def send(v, move):
        return lax.ppermute(v, axes, device_pairs(groups, move))

    def along_x(v, which, by):
        return send(v, lambda g, u, t: (g, u, t + by) if g % 2 == which else None)

    def table(pairs):
        up = jnp.array([k for k, d in pairs], jnp.int32)
        along = jnp.array([d for k, d in pairs], jnp.int32)
        src = ((z + NZ - up) % NZ) * NX + (x + NX - along) % NX
        return jnp.concatenate([core.reshape(1), src]).astype(jnp.int32)

    halves = ((0, 1), (2, 3))
    meta_a = table([(k, d) for h in halves for d in DX for k in h])
    meta_b = table([(k, d) for d in DX for k in range(NZ)])

    def ahead_by(v):
        return send(v, lambda g, u, t: (g, u + 1, t))

    def fan(v, which):
        out = [v]
        for d in DX[1:]:
            out.append(along_x(v, which, d))
        return out

    def swap(v):
        return send(v, lambda g, u, t: (g + 1 - 2 * (g % 2), u, t))

    w = pack_weights(w_gate[0], w_up[0])
    r1 = ahead_by(own)
    r2 = ahead_by(r1)
    first = cat([own, r1])
    ahead = fan(first, 0)
    r3 = ahead_by(r2)
    hg = split_units(hidden_grad[0], NZ * NX, r2)
    hg = lax.all_to_all(hg, "dp", split_axis=0, concat_axis=0, tiled=True)
    second = cat([r2, r3])
    behind = fan(second, 0)

    step_a, cross_a = [], []
    for c in range(CHUNKS):
        step_a.append(step_chunk(0, c, meta_a, hg, w, ahead + behind))
        cross_a.append(send(step_a[c], lambda g, u, t: (g - 1, u, t) if g % 2 == 0 else None))

    token = swap(step_a[0][:8, :128])
    block = cat([first, second], token, *step_a)
    blocks = fan(block, 1)
    mine, cross_b, near = [], [], []
    for c in range(CHUNKS):
        mine.append(step_chunk(1, c, meta_b, hg, w, blocks, step_a[c]))
        cross_b.append(send(mine[c], lambda g, u, t: (g + 1, u, t) if g % 2 == 1 else None))
        near.append(swap(mine[c]))

    done = None
    for c in range(CHUNKS):
        done = mix_chunk(c, meta_a, mine[c], near[c], cross_a[c], cross_b[c], done)
    return done[0][None], done[1][None]


def solution(mesh):
    in_specs = (
        P("grp", "dp", None),
        P("grp", "dp", None),
        P("grp", None, "dp"),
        P("grp", None, "dp"),
    )
    out_specs = (P("grp", None, "dp"), P("grp", None, "dp"))

    return jax.shard_map(local, mesh=mesh, in_specs=in_specs, out_specs=out_specs, check_vma=False)
```

time: 322 us -> 289 us (0.90)
  waiting for transfers between devices: 254 us -> 132 us
  starting transfers between devices: 16.4 us -> 105 us
  Pallas kernels: 0 us -> 39.2 us
  matrix products: 24.8 us -> 0 us
  between operations: 14.1 us -> 1.04 us
    all_to_all x1, waiting for transfers between devices: 109 us -> 0.01 us  [local(): hg = lax.all_to_all(hg, 'dp', split_axis=0, concat_axis=0, tiled=True)]
    ppermute x2 -> x22, starting transfers between devices: 7.83 us -> 97.3 us  [send(): return lax.ppermute(v, axes, device_pairs(groups, move))]
    pallas_call x0 -> x14, Pallas kernels: none -> 39.2 us  [the longest x6 29.2 us: step_chunk(): pl.pallas_call(functools.partial(step_body, which, len(xs)), grid=(1,), o...]
    dot_general x3 -> x0, matrix products: 24.8 us -> none  [the longest x1 9.29 us: gating(): jnp.dot(rows, gate_weight, preferred_element_type=jnp.float32) * scale]
    all_gather x1 -> x0, waiting for transfers between devices: 8.11 us -> none  [local(): gathered = lax.all_gather(local_rows, 'dp', axis=0, tiled=True)]
    ppermute x2 -> x22, waiting for transfers between devices: 136 us -> 132 us  [send(): return lax.ppermute(v, axes, device_pairs(groups, move))]
    unnamed x15 -> x24, local copies, waits for them, and re-layouts: 8.12 us -> 8.72 us
  transfers between devices with their start and end apart: 4 -> 23, of which waited for: 3 -> 8; matrix products, arithmetic and copies ran while one was open for 2% -> 0% of each run, Pallas kernels for 0% -> 9%
where the time goes in v1:
time: 289 us; the launch traced here: 286 us
  waiting for transfers between devices  132 us (46%)
  starting transfers between devices  105 us (36%)
  Pallas kernels  39.2 us (14%)
  local copies, waits for them, and re-layouts  8.72 us (3%)
    ppermute x22, waiting for transfers between devices, send(): return lax.ppermute(v, axes, device_pairs(groups, move))  132 us
    ppermute x22, starting transfers between devices, send(): return lax.ppermute(v, axes, device_pairs(groups, move))  97.3 us
    pallas_call x6, Pallas kernels, step_chunk(): pl.pallas_call(functools.partial(step_body, which, len(xs)), grid=(1,), o...  29.2 us
    unnamed x24, local copies, waits for them, and re-layouts  8.72 us
    all_to_all x1, starting transfers between devices, local(): hg = lax.all_to_all(hg, 'dp', split_axis=0, concat_axis=0, tiled=True)  7.9 us
    pallas_call x3, Pallas kernels, mix_chunk(): pl.pallas_call(mix_body, grid=(width // band,), out_shape=(jax.ShapeDtype...  7.29 us
  transfers between devices with their start and end apart: 23, of which 8 were waited for; matrix products, arithmetic and copies ran while one was open for 0% of the time, Pallas kernels for 9%

profile of v1, /device:TPU:38, one launch (start us, length us, event | category | flops | bytes accessed | tf_op | source)
XLA Modules:
  0.0 286.2 jit_solution(15628777584924896459)
XLA Ops:
  0.6 2.0 collective-permute-start
  2.6 12.0 %collective-permute-done.refs_1_ = bf16[128,2048]{1,0:T(8,128)(2,1)S(1)} collective-permute-done((bf16[128,2048]{1,0:T(8,128)(2,1)}, bf16[128,2048]{1,0:T(8,128)(2,1)S(1)}, u32[]{:S(2)}, u32[]{:S(2)}) %collective-permute-start) | collective-permute-done | bytes 524320 | tf_op jit(solution)/shard_map/ppermute | solution.py:228
  14.6 1.9 collective-permute-start.1
  16.5 12.4 %collective-permute-done.1.refs_0_ = bf16[128,2048]{1,0:T(8,128)(2,1)S(1)} collective-permute-done((bf16[128,2048]{1,0:T(8,128)(2,1)S(1)}, bf16[128,2048]{1,0:T(8,128)(2,1)S(1)}, u32[]{:S(2)}, u32[]{:S(2)}) %collective-permute-start.1) | collective-permute-done | bytes 524320 | tf_op jit(solution)/shard_map/ppermute | solution.py:228
  28.9 1.4 copy-done.2
  30.3 1.3 split.1
  31.6 7.9 %all-to-all-start = ((bf16[16,128,384]{2,1,0:T(8,128)(2,1)}), bf16[16,128,384]{2,1,0:T(8,128)(2,1)}, u32[]{:S(2)}, u32[]{:S(2)}) async-start(bf16[16,128,384]{2,1,0:T(8,128)(2,1)} %split.1), calls=%async_computation | async-start | bytes 3145728 | tf_op jit(solution)/shard_map/all_to_all | solution.py:262
  39.5 0.1 cat.3.refs_0_
  39.6 3.4 %collective-permute-start.5 = (bf16[256,2048]{1,0:T(8,128)(2,1)S(1)}, bf16[256,2048]{1,0:T(8,128)(2,1)S(1)}, u32[]{:S(2)}, u32[]{:S(2)}) collective-permute-start(bf16[256,2048]{1,0:T(8,128)(2,1)S(1)} %cat.3.refs_0_), channel_id=1, source_target_pairs={{0,2},{1,3},{2,0},{3,1},{4,6},{5,7},{6,4},{7,5},{8,10},{9,11},{10,... | collective-permute-start | bytes 3145736 | tf_op jit(solution)/shard_map/ppermute | solution.py:228
  43.0 1.5 collective-permute-start.2
  44.5 1.9 collective-permute-start.4
  46.5 5.1 %collective-permute-start.3 = (bf16[256,2048]{1,0:T(8,128)(2,1)S(1)}, bf16[256,2048]{1,0:T(8,128)(2,1)}, u32[]{:S(2)}, u32[]{:S(2)}) collective-permute-start(bf16[256,2048]{1,0:T(8,128)(2,1)S(1)} %cat.3.refs_0_), channel_id=1, source_target_pairs={{0,1},{1,2},{2,3},{3,0},{4,5},{5,6},{6,7},{7,4},{8,9},{9,10},{10,1... | collective-permute-start | bytes 3145736 | tf_op jit(solution)/shard_map/ppermute | solution.py:228
  51.6 31.3 %collective-permute-done.2.refs_1_ = bf16[128,2048]{1,0:T(8,128)(2,1)S(1)} collective-permute-done((bf16[128,2048]{1,0:T(8,128)(2,1)S(1)}, bf16[128,2048]{1,0:T(8,128)(2,1)S(1)}, u32[]{:S(2)}, u32[]{:S(2)}) %collective-permute-start.2) | collective-permute-done | bytes 524320 | tf_op jit(solution)/shard_map/ppermute | solution.py:228
  82.9 0.1 cat.4.refs_4_.refs_1_
  83.0 4.0 %collective-permute-start.8 = (bf16[256,2048]{1,0:T(8,128)(2,1)S(1)}, bf16[256,2048]{1,0:T(8,128)(2,1)}, u32[]{:S(2)}, u32[]{:S(2)}) collective-permute-start(bf16[256,2048]{1,0:T(8,128)(2,1)S(1)} %cat.4.refs_4_.refs_1_), channel_id=1, source_target_pairs={{0,2},{1,3},{2,0},{3,1},{4,6},{5,7},{6,4},{7,5},{8,10},{9,11},{10,... | collective-permute-start | bytes 3145736 | tf_op jit(solution)/shard_map/ppermute | solution.py:228
  87.0 1.9 collective-permute-start.7
  88.9 0.0 copy-start.6
  88.9 1.0 copy-done.6
  89.9 5.1 %collective-permute-start.6 = (bf16[256,2048]{1,0:T(8,128)(2,1)S(1)}, bf16[256,2048]{1,0:T(8,128)(2,1)}, u32[]{:S(2)}, u32[]{:S(2)}) collective-permute-start(bf16[256,2048]{1,0:T(8,128)(2,1)S(1)} %cat.4.refs_4_.refs_1_), channel_id=1, source_target_pairs={{0,1},{1,2},{2,3},{3,0},{4,5},{5,6},{6,7},{7,4},{8,9},{9,10},{10,1... | collective-permute-start | bytes 3145736 | tf_op jit(solution)/shard_map/ppermute | solution.py:228
  95.1 0.0 copy-start.3
  95.1 1.4 copy-done.3
  96.5 1.4 copy-done.4
  97.9 1.2 pack.1.w
  99.1 1.6 copy-done
  100.7 0.1 pad_add_fusion.meta
  100.8 0.6 collective-permute-done.8.refs_7_
  101.4 11.1 %collective-permute-done.7.refs_6_ = bf16[256,2048]{1,0:T(8,128)(2,1)} collective-permute-done((bf16[256,2048]{1,0:T(8,128)(2,1)S(1)}, bf16[256,2048]{1,0:T(8,128)(2,1)}, u32[]{:S(2)}, u32[]{:S(2)}) %collective-permute-start.7) | collective-permute-done | bytes 1048608 | tf_op jit(solution)/shard_map/ppermute | solution.py:228
  112.6 1.9 copy-done.1
  114.4 8.5 %step.6.refs_3_.refs_4_ = bf16[2048,256]{1,0:T(8,128)(2,1)S(1)} custom-call(s32[17]{0:T(128)S(1)} %pad_add_fusion.meta, bf16[16,128,384]{2,1,0:T(8,128)(2,1)} %all-to-all-done.hg, bf16[3,2048,256]{2,1,0:T(8,128)(2,1)S(1)} %copy-done.1, bf16[256,2048]{1,0:T(8,128)(2,1)S(1)} %cat.3.refs_0_, bf16[256,2048]{1,0:T(8,128)(2,1)} %collective-permute-done.3.refs_1_, ...), custom_call_target="tpu_custom_call" | custom-call | flops 4294967296 | bytes 8388608 | tf_op jit(solution)/shard_map/step/pallas_call | solution.py:158
  123.0 0.1 collective-permute-start.9
  123.1 8.5 %step.8.refs_5_.refs_4_ = bf16[2048,256]{1,0:T(8,128)(2,1)S(1)} custom-call(s32[17]{0:T(128)S(1)} %pad_add_fusion.meta, bf16[16,128,384]{2,1,0:T(8,128)(2,1)} %all-to-all-done.hg, bf16[3,2048,256]{2,1,0:T(8,128)(2,1)S(1)} %copy-done.1, bf16[256,2048]{1,0:T(8,128)(2,1)S(1)} %cat.3.refs_0_, bf16[256,2048]{1,0:T(8,128)(2,1)} %collective-permute-done.3.refs_1_, ...), custom_call_target="tpu_custom_call" | custom-call | flops 4294967296 | bytes 8388608 | tf_op jit(solution)/shard_map/step/pallas_call | solution.py:158
  131.6 8.5 %step.7.refs_4_ = bf16[2048,256]{1,0:T(8,128)(2,1)S(1)} custom-call(s32[17]{0:T(128)S(1)} %pad_add_fusion.meta, bf16[16,128,384]{2,1,0:T(8,128)(2,1)} %all-to-all-done.hg, bf16[3,2048,256]{2,1,0:T(8,128)(2,1)S(1)} %copy-done.1, bf16[256,2048]{1,0:T(8,128)(2,1)S(1)} %cat.3.refs_0_, bf16[256,2048]{1,0:T(8,128)(2,1)} %collective-permute-done.3.refs_1_, ...), custom_call_target="tpu_custom_call" | custom-call | flops 4294967296 | bytes 8388608 | tf_op jit(solution)/shard_map/step/pallas_call | solution.py:158
  140.2 0.0 copy-start.8
  140.2 0.0 copy-start.9
  140.2 0.0 collective-permute-done.9.refs_2_
  140.2 0.2 cat.5.refs_0_
  140.4 0.8 collective-permute-start.12
  141.2 0.8 collective-permute-start.11
  142.0 0.8 collective-permute-start.10
  142.9 0.1 pad_add_fusion.1.meta
  142.9 3.2 %collective-permute-start.17 = (bf16[2048,256]{1,0:T(8,128)(2,1)S(1)}, bf16[2048,256]{1,0:T(8,128)(2,1)S(1)}, u32[]{:S(2)}, u32[]{:S(2)}) collective-permute-start(bf16[2048,256]{1,0:T(8,128)(2,1)S(1)} %step.7.refs_4_), channel_id=1, source_target_pairs={{0,240},{1,241},{2,242},{3,243},{4,244},{5,245},{6,246},{7,247},{8... | collective-permute-start | bytes 3145736 | tf_op jit(solution)/shard_map/ppermute | solution.py:228
  146.2 1.4 collective-permute-start.20
  147.5 0.0 collective-permute-done.12.refs_3_
  147.5 0.0 collective-permute-done.11.refs_2_
  147.6 1.2 step.11.own
  148.7 1.5 collective-permute-start.21
  150.2 36.0 %collective-permute-start.19 = (bf16[2048,256]{1,0:T(8,128)(2,1)S(1)}, bf16[2048,256]{1,0:T(8,128)(2,1)S(1)}, u32[]{:S(2)}, u32[]{:S(2)}) collective-permute-start(bf16[2048,256]{1,0:T(8,128)(2,1)S(1)} %step.11.own), channel_id=1, source_target_pairs={{0,16},{1,17},{2,18},{3,19},{4,20},{5,21},{6,22},{7,23},{8,24},{9,... | collective-permute-start | bytes 3145736 | tf_op jit(solution)/shard_map/ppermute | solution.py:228
  186.2 1.2 step.10.own
  187.4 1.3 collective-permute-start.18
  188.7 1.2 step.9.own
  189.9 0.0 collective-permute-done.17.far_a
  189.9 13.5 %collective-permute-start.16 = (bf16[2048,256]{1,0:T(8,128)(2,1)S(1)}, bf16[2048,256]{1,0:T(8,128)(2,1)S(1)}, u32[]{:S(2)}, u32[]{:S(2)}) collective-permute-start(bf16[2048,256]{1,0:T(8,128)(2,1)S(1)} %step.10.own), channel_id=1, source_target_pairs={{0,16},{1,17},{2,18},{3,19},{4,20},{5,21},{6,22},{7,23},{8,24},{9,... | collective-permute-start | bytes 3145736 | tf_op jit(solution)/shard_map/ppermute | solution.py:228
  203.4 9.7 %collective-permute-start.14 = (bf16[2048,256]{1,0:T(8,128)(2,1)S(1)}, bf16[2048,256]{1,0:T(8,128)(2,1)S(1)}, u32[]{:S(2)}, u32[]{:S(2)}) collective-permute-start(bf16[2048,256]{1,0:T(8,128)(2,1)S(1)} %step.8.refs_5_.refs_4_), channel_id=1, source_target_pairs={{0,240},{1,241},{2,242},{3,243},{4,244},{5,245},{6,246},{7,247},{8... | collective-permute-start | bytes 3145736 | tf_op jit(solution)/shard_map/ppermute | solution.py:228
  213.1 1.3 collective-permute-start.15
  214.4 0.0 collective-permute-done.19.near
  214.4 0.1 collective-permute-start.13
  214.5 2.5 mix.3
  217.0 21.0 %collective-permute-done.18.far_b = bf16[2048,256]{1,0:T(8,128)(2,1)S(1)} collective-permute-done((bf16[2048,256]{1,0:T(8,128)(2,1)S(1)}, bf16[2048,256]{1,0:T(8,128)(2,1)S(1)}, u32[]{:S(2)}, u32[]{:S(2)}) %collective-permute-start.18) | collective-permute-done | bytes 1048608 | tf_op jit(solution)/shard_map/ppermute | solution.py:228
  238.1 0.0 collective-permute-done.16.near
  238.1 2.4 mix.4
  240.5 5.3 %collective-permute-done.14.far_a = bf16[2048,256]{1,0:T(8,128)(2,1)S(1)} collective-permute-done((bf16[2048,256]{1,0:T(8,128)(2,1)S(1)}, bf16[2048,256]{1,0:T(8,128)(2,1)S(1)}, u32[]{:S(2)}, u32[]{:S(2)}) %collective-permute-start.14) | collective-permute-done | bytes 1048608 | tf_op jit(solution)/shard_map/ppermute | solution.py:228
  245.8 38.0 %collective-permute-done.15.far_b = bf16[2048,256]{1,0:T(8,128)(2,1)S(1)} collective-permute-done((bf16[2048,256]{1,0:T(8,128)(2,1)S(1)}, bf16[2048,256]{1,0:T(8,128)(2,1)S(1)}, u32[]{:S(2)}, u32[]{:S(2)}) %collective-permute-start.15) | collective-permute-done | bytes 1048608 | tf_op jit(solution)/shard_map/ppermute | solution.py:228
  283.8 0.0 collective-permute-done.13.near
  283.8 2.4 mix.5
  (25 shorter events, 0.1 us)
Async XLA Ops:
  0.6 14.0 %collective-permute-start = (bf16[128,2048]{1,0:T(8,128)(2,1)}, bf16[128,2048]{1,0:T(8,128)(2,1)S(1)}, u32[]{:S(2)}, u32[]{:S(2)}) collective-permute-start(bf16[128,2048]{1,0:T(8,128)(2,1)} %bitcast.10), channel_id=1, source_target_pairs={{0,4},{1,5},{2,6},{3,7},{4,8},{5,9},{6,10},{7,11},{8,12},{9,13},{1... | collective-permute-start | bytes 1572872 | tf_op jit(solution)/shard_map/ppermute | solution.py:228
  14.6 14.3 %collective-permute-start.1 = (bf16[128,2048]{1,0:T(8,128)(2,1)S(1)}, bf16[128,2048]{1,0:T(8,128)(2,1)S(1)}, u32[]{:S(2)}, u32[]{:S(2)}) collective-permute-start(bf16[128,2048]{1,0:T(8,128)(2,1)S(1)} %collective-permute-done.refs_1_), channel_id=1, source_target_pairs={{0,4},{1,5},{2,6},{3,7},{4,8},{5,9},{6,10},{7,11},{8,12},{9,13},{1... | collective-permute-start | bytes 1572872 | tf_op jit(solution)/shard_map/ppermute | solution.py:228
  28.9 1.4 copy-start.2
  31.6 7.9 %copy-start.5 = (bf16[1,128,2048]{2,1,0:T(8,128)(2,1)S(1)}, bf16[1,128,2048]{2,1,0:T(8,128)(2,1)}, u32[]{:S(2)}) copy-start(bf16[1,128,2048]{2,1,0:T(8,128)(2,1)} %param.8) | copy-start | bytes 1572868
  31.6 80.9 %all-to-all-start = ((bf16[16,128,384]{2,1,0:T(8,128)(2,1)}), bf16[16,128,384]{2,1,0:T(8,128)(2,1)}, u32[]{:S(2)}, u32[]{:S(2)}) async-start(bf16[16,128,384]{2,1,0:T(8,128)(2,1)} %split.1), calls=%async_computation | async-start | bytes 3145728 | tf_op jit(solution)/shard_map/all_to_all | solution.py:262
  39.6 49.3 %collective-permute-start.5 = (bf16[256,2048]{1,0:T(8,128)(2,1)S(1)}, bf16[256,2048]{1,0:T(8,128)(2,1)S(1)}, u32[]{:S(2)}, u32[]{:S(2)}) collective-permute-start(bf16[256,2048]{1,0:T(8,128)(2,1)S(1)} %cat.3.refs_0_), channel_id=1, source_target_pairs={{0,2},{1,3},{2,0},{3,1},{4,6},{5,7},{6,4},{7,5},{8,10},{9,11},{10,... | collective-permute-start | bytes 3145736 | tf_op jit(solution)/shard_map/ppermute | solution.py:228
  43.0 39.9 %collective-permute-start.2 = (bf16[128,2048]{1,0:T(8,128)(2,1)S(1)}, bf16[128,2048]{1,0:T(8,128)(2,1)S(1)}, u32[]{:S(2)}, u32[]{:S(2)}) collective-permute-start(bf16[128,2048]{1,0:T(8,128)(2,1)S(1)} %collective-permute-done.1.refs_0_), channel_id=1, source_target_pairs={{0,4},{1,5},{2,6},{3,7},{4,8},{5,9},{6,10},{7,11},{8,12},{9,13},{1... | collective-permute-start | bytes 1572872 | tf_op jit(solution)/shard_map/ppermute | solution.py:228
  44.5 56.2 %collective-permute-start.4 = (bf16[256,2048]{1,0:T(8,128)(2,1)S(1)}, bf16[256,2048]{1,0:T(8,128)(2,1)}, u32[]{:S(2)}, u32[]{:S(2)}) collective-permute-start(bf16[256,2048]{1,0:T(8,128)(2,1)S(1)} %cat.3.refs_0_), channel_id=1, source_target_pairs={{0,3},{1,0},{2,1},{3,2},{4,7},{5,4},{6,5},{7,6},{8,11},{9,8},{10,9... | collective-permute-start | bytes 3145736 | tf_op jit(solution)/shard_map/ppermute | solution.py:228
  46.5 54.3 %collective-permute-start.3 = (bf16[256,2048]{1,0:T(8,128)(2,1)S(1)}, bf16[256,2048]{1,0:T(8,128)(2,1)}, u32[]{:S(2)}, u32[]{:S(2)}) collective-permute-start(bf16[256,2048]{1,0:T(8,128)(2,1)S(1)} %cat.3.refs_0_), channel_id=1, source_target_pairs={{0,1},{1,2},{2,3},{3,0},{4,5},{5,6},{6,7},{7,4},{8,9},{9,10},{10,1... | collective-permute-start | bytes 3145736 | tf_op jit(solution)/shard_map/ppermute | solution.py:228
  83.0 18.4 %collective-permute-start.8 = (bf16[256,2048]{1,0:T(8,128)(2,1)S(1)}, bf16[256,2048]{1,0:T(8,128)(2,1)}, u32[]{:S(2)}, u32[]{:S(2)}) collective-permute-start(bf16[256,2048]{1,0:T(8,128)(2,1)S(1)} %cat.4.refs_4_.refs_1_), channel_id=1, source_target_pairs={{0,2},{1,3},{2,0},{3,1},{4,6},{5,7},{6,4},{7,5},{8,10},{9,11},{10,... | collective-permute-start | bytes 3145736 | tf_op jit(solution)/shard_map/ppermute | solution.py:228
  87.0 25.5 %collective-permute-start.7 = (bf16[256,2048]{1,0:T(8,128)(2,1)S(1)}, bf16[256,2048]{1,0:T(8,128)(2,1)}, u32[]{:S(2)}, u32[]{:S(2)}) collective-permute-start(bf16[256,2048]{1,0:T(8,128)(2,1)S(1)} %cat.4.refs_4_.refs_1_), channel_id=1, source_target_pairs={{0,3},{1,0},{2,1},{3,2},{4,7},{5,4},{6,5},{7,6},{8,11},{9,8},{10,9... | collective-permute-start | bytes 3145736 | tf_op jit(solution)/shard_map/ppermute | solution.py:228
  88.9 1.0 copy-start.6
  89.9 22.6 %collective-permute-start.6 = (bf16[256,2048]{1,0:T(8,128)(2,1)S(1)}, bf16[256,2048]{1,0:T(8,128)(2,1)}, u32[]{:S(2)}, u32[]{:S(2)}) collective-permute-start(bf16[256,2048]{1,0:T(8,128)(2,1)S(1)} %cat.4.refs_4_.refs_1_), channel_id=1, source_target_pairs={{0,1},{1,2},{2,3},{3,0},{4,5},{5,6},{6,7},{7,4},{8,9},{9,10},{10,1... | collective-permute-start | bytes 3145736 | tf_op jit(solution)/shard_map/ppermute | solution.py:228
  95.1 1.4 copy-start.3
  96.5 1.4 copy-start.4
  97.9 2.8 copy-start.10
  97.9 2.8 copy-start.11
  97.9 14.7 %copy-start.7 = (bf16[256,2048]{1,0:T(8,128)(2,1)S(1)}, bf16[256,2048]{1,0:T(8,128)(2,1)}, u32[]{:S(2)}) copy-start(bf16[256,2048]{1,0:T(8,128)(2,1)} %copy-done.6) | copy-start | bytes 3145732
  99.0 1.6 copy-start
  112.5 1.9 copy-start.1
  123.0 17.2 %collective-permute-start.9 = (bf16[8,128]{1,0:T(8,128)(2,1)S(1)}, bf16[8,128]{1,0:T(8,128)(2,1)S(1)}, u32[]{:S(2)}, u32[]{:S(2)}) collective-permute-start(bf16[8,128]{1,0:T(8,128)(2,1)S(1)} %slice.4), channel_id=1, source_target_pairs={{0,16},{1,17},{2,18},{3,19},{4,20},{5,21},{6,22},{7,23},{8,24},{9,... | collective-permute-start | bytes 6152 | tf_op jit(solution)/shard_map/ppermute | solution.py:228
  140.2 2.6 copy-start.8
  140.2 2.6 copy-start.9
  140.4 7.1 %collective-permute-start.12 = (bf16[512,2048]{1,0:T(8,128)(2,1)S(1)}, bf16[512,2048]{1,0:T(8,128)(2,1)S(1)}, u32[]{:S(2)}, u32[]{:S(2)}) collective-permute-start(bf16[512,2048]{1,0:T(8,128)(2,1)S(1)} %cat.5.refs_0_), channel_id=1, source_target_pairs={{16,18},{17,19},{18,16},{19,17},{20,22},{21,23},{22,20},{23,21},{2... | collective-permute-start | bytes 6291464 | tf_op jit(solution)/shard_map/ppermute | solution.py:228
  141.2 6.3 %collective-permute-start.11 = (bf16[512,2048]{1,0:T(8,128)(2,1)S(1)}, bf16[512,2048]{1,0:T(8,128)(2,1)S(1)}, u32[]{:S(2)}, u32[]{:S(2)}) collective-permute-start(bf16[512,2048]{1,0:T(8,128)(2,1)S(1)} %cat.5.refs_0_), channel_id=1, source_target_pairs={{16,19},{17,16},{18,17},{19,18},{20,23},{21,20},{22,21},{23,22},{2... | collective-permute-start | bytes 6291464 | tf_op jit(solution)/shard_map/ppermute | solution.py:228
  142.0 5.5 %collective-permute-start.10 = (bf16[512,2048]{1,0:T(8,128)(2,1)S(1)}, bf16[512,2048]{1,0:T(8,128)(2,1)S(1)}, u32[]{:S(2)}, u32[]{:S(2)}) collective-permute-start(bf16[512,2048]{1,0:T(8,128)(2,1)S(1)} %cat.5.refs_0_), channel_id=1, source_target_pairs={{16,17},{17,18},{18,19},{19,16},{20,21},{21,22},{22,23},{23,20},{2... | collective-permute-start | bytes 6291464 | tf_op jit(solution)/shard_map/ppermute | solution.py:228
  142.9 46.9 %collective-permute-start.17 = (bf16[2048,256]{1,0:T(8,128)(2,1)S(1)}, bf16[2048,256]{1,0:T(8,128)(2,1)S(1)}, u32[]{:S(2)}, u32[]{:S(2)}) collective-permute-start(bf16[2048,256]{1,0:T(8,128)(2,1)S(1)} %step.7.refs_4_), channel_id=1, source_target_pairs={{0,240},{1,241},{2,242},{3,243},{4,244},{5,245},{6,246},{7,247},{8... | collective-permute-start | bytes 3145736 | tf_op jit(solution)/shard_map/ppermute | solution.py:228
  146.2 57.2 %collective-permute-start.20 = (bf16[2048,256]{1,0:T(8,128)(2,1)S(1)}, bf16[2048,256]{1,0:T(8,128)(2,1)S(1)}, u32[]{:S(2)}, u32[]{:S(2)}) collective-permute-start(bf16[2048,256]{1,0:T(8,128)(2,1)S(1)} %step.6.refs_3_.refs_4_), channel_id=1, source_target_pairs={{0,240},{1,241},{2,242},{3,243},{4,244},{5,245},{6,246},{7,247},{8... | collective-permute-start | bytes 3145736 | tf_op jit(solution)/shard_map/ppermute | solution.py:228
  148.7 64.4 %collective-permute-start.21 = (bf16[2048,256]{1,0:T(8,128)(2,1)S(1)}, bf16[2048,256]{1,0:T(8,128)(2,1)S(1)}, u32[]{:S(2)}, u32[]{:S(2)}) collective-permute-start(bf16[2048,256]{1,0:T(8,128)(2,1)S(1)} %step.11.own), channel_id=1, source_target_pairs={{16,32},{17,33},{18,34},{19,35},{20,36},{21,37},{22,38},{23,39},{2... | collective-permute-start | bytes 3145736 | tf_op jit(solution)/shard_map/ppermute | solution.py:228
  150.2 64.2 %collective-permute-start.19 = (bf16[2048,256]{1,0:T(8,128)(2,1)S(1)}, bf16[2048,256]{1,0:T(8,128)(2,1)S(1)}, u32[]{:S(2)}, u32[]{:S(2)}) collective-permute-start(bf16[2048,256]{1,0:T(8,128)(2,1)S(1)} %step.11.own), channel_id=1, source_target_pairs={{0,16},{1,17},{2,18},{3,19},{4,20},{5,21},{6,22},{7,23},{8,24},{9,... | collective-permute-start | bytes 3145736 | tf_op jit(solution)/shard_map/ppermute | solution.py:228
  187.4 50.7 %collective-permute-start.18 = (bf16[2048,256]{1,0:T(8,128)(2,1)S(1)}, bf16[2048,256]{1,0:T(8,128)(2,1)S(1)}, u32[]{:S(2)}, u32[]{:S(2)}) collective-permute-start(bf16[2048,256]{1,0:T(8,128)(2,1)S(1)} %step.10.own), channel_id=1, source_target_pairs={{16,32},{17,33},{18,34},{19,35},{20,36},{21,37},{22,38},{23,39},{2... | collective-permute-start | bytes 3145736 | tf_op jit(solution)/shard_map/ppermute | solution.py:228
  189.9 48.2 %collective-permute-start.16 = (bf16[2048,256]{1,0:T(8,128)(2,1)S(1)}, bf16[2048,256]{1,0:T(8,128)(2,1)S(1)}, u32[]{:S(2)}, u32[]{:S(2)}) collective-permute-start(bf16[2048,256]{1,0:T(8,128)(2,1)S(1)} %step.10.own), channel_id=1, source_target_pairs={{0,16},{1,17},{2,18},{3,19},{4,20},{5,21},{6,22},{7,23},{8,24},{9,... | collective-permute-start | bytes 3145736 | tf_op jit(solution)/shard_map/ppermute | solution.py:228
  203.4 42.4 %collective-permute-start.14 = (bf16[2048,256]{1,0:T(8,128)(2,1)S(1)}, bf16[2048,256]{1,0:T(8,128)(2,1)S(1)}, u32[]{:S(2)}, u32[]{:S(2)}) collective-permute-start(bf16[2048,256]{1,0:T(8,128)(2,1)S(1)} %step.8.refs_5_.refs_4_), channel_id=1, source_target_pairs={{0,240},{1,241},{2,242},{3,243},{4,244},{5,245},{6,246},{7,247},{8... | collective-permute-start | bytes 3145736 | tf_op jit(solution)/shard_map/ppermute | solution.py:228
  213.1 70.7 %collective-permute-start.15 = (bf16[2048,256]{1,0:T(8,128)(2,1)S(1)}, bf16[2048,256]{1,0:T(8,128)(2,1)S(1)}, u32[]{:S(2)}, u32[]{:S(2)}) collective-permute-start(bf16[2048,256]{1,0:T(8,128)(2,1)S(1)} %step.9.own), channel_id=1, source_target_pairs={{16,32},{17,33},{18,34},{19,35},{20,36},{21,37},{22,38},{23,39},{2... | collective-permute-start | bytes 3145736 | tf_op jit(solution)/shard_map/ppermute | solution.py:228
  214.4 69.4 %collective-permute-start.13 = (bf16[2048,256]{1,0:T(8,128)(2,1)S(1)}, bf16[2048,256]{1,0:T(8,128)(2,1)S(1)}, u32[]{:S(2)}, u32[]{:S(2)}) collective-permute-start(bf16[2048,256]{1,0:T(8,128)(2,1)S(1)} %step.9.own), channel_id=1, source_target_pairs={{0,16},{1,17},{2,18},{3,19},{4,20},{5,21},{6,22},{7,23},{8,24},{9,... | collective-permute-start | bytes 3145736 | tf_op jit(solution)/shard_map/ppermute | solution.py:228

commit v2 on v1

--- a/solution.py
+++ b/solution.py
@@ -35,23 +35,25 @@
     return out
 
 
-def split_body(hg, *refs):
-    out = refs[-1]
+def split_body(hg, out, sem):
     units = out.shape[2]
     for i in range(out.shape[0]):
-        out[i] = hg[:, i * units:(i + 1) * units]
-
-
-def split_units(hg, parts, *deps):
+        pltpu.make_async_copy(hg.at[:, i * units:(i + 1) * units], out.at[i], sem.at[i]).start()
+    for i in range(out.shape[0]):
+        pltpu.make_async_copy(hg.at[:, i * units:(i + 1) * units], out.at[i], sem.at[i]).wait()
+
+
+def split_units(hg, parts):
     rows, width = hg.shape
     return pl.pallas_call(
         split_body,
         out_shape=jax.ShapeDtypeStruct((parts, rows, width // parts), hg.dtype),
-        in_specs=[VMEM] + [HBM] * len(deps),
-        out_specs=VMEM,
-        compiler_params=params(8),
+        in_specs=[HBM],
+        out_specs=HBM,
+        scratch_shapes=[pltpu.SemaphoreType.DMA((parts,))],
+        compiler_params=params(4),
         name="split",
-    )(hg, *deps)
+    )(hg)
 
 
 def pack_body(g, u, out):
@@ -73,6 +75,33 @@
         compiler_params=params(10),
         name="pack",
     )(g, u)
+
+
+def pick_body(meta, own, got, a, b, sems):
+    half = a.shape[0]
+    for core in range(2):
+        @pl.when(meta[0] == core)
+        def _():
+            at = pl.ds(core * half, half)
+            ca = pltpu.make_async_copy((own if core == 0 else got).at[at], a, sems.at[0])
+            cb = pltpu.make_async_copy((got if core == 0 else own).at[at], b, sems.at[1])
+            ca.start()
+            cb.start()
+            ca.wait()
+            cb.wait()
+
+
+def pick(meta, own, got):
+    shape = jax.ShapeDtypeStruct((own.shape[0] // 2, own.shape[1]), own.dtype)
+    return pl.pallas_call(
+        pick_body,
+        out_shape=(shape, shape),
+        in_specs=[SMEM, HBM, HBM],
+        out_specs=(HBM, HBM),
+        scratch_shapes=[pltpu.SemaphoreType.DMA((2,))],
+        compiler_params=params(4),
+        name="pick",
+    )(meta, own, got)
 
 
 def cat_body(count, *refs):
@@ -100,32 +129,43 @@
     )(*xs, *deps)
 
 
-def step_body(which, count, meta, hg, w, *refs):
+def step_body(which, count, c, meta, units, packed, *refs):
     xs = refs[:count]
     rest = refs[count:]
     other = rest[0] if which == 1 else None
-    out, x, rows, sems = rest[-4:]
-    uw = w.shape[2] // 2
-    blk = hg.shape[1]
+    out, x, w, hg, rows, sems = rest[-6:]
+    uw = w.shape[1] // 2
+    blk = hg.shape[1] // 2
     part = 512
-    scale = w.shape[1] ** (-0.5)
+    scale = w.shape[0] ** (-0.5)
 
     @pl.when(meta[0] == which)
     def _():
+        weights = pltpu.make_async_copy(packed.at[c], w, sems.at[x.shape[0] // part])
+        weights.start()
+        cotangents = pltpu.make_async_copy(units.at[:, :, c * uw:(c + 1) * uw], hg, sems.at[x.shape[0] // part + 1])
+        cotangents.start()
         at = 0
         for v in xs:
-            pltpu.make_async_copy(v, x.at[pl.ds(at, v.shape[0])], sems.at[at // part]).start()
-            at += v.shape[0]
+            done = 0
+            while done < v.shape[0]:
+                n = min(part - at % part, v.shape[0] - done)
+                pltpu.make_async_copy(v.at[pl.ds(done, n)], x.at[pl.ds(at, n)], sems.at[at // part]).start()
+                at += n
+                done += n
+        weights.wait()
+        cotangents.wait()
 
         def products(i, carry):
             at = pl.multiple_of(i * part, part)
             here = x.at[pl.ds(at, part)]
             pltpu.make_async_copy(here, here, sems.at[i]).wait()
-            gu = jnp.dot(x[pl.ds(at, part), :], w[0], preferred_element_type=jnp.float32) * scale
+            half = pl.multiple_of(jnp.where(i < 2, which, 1 - which) * blk, blk)
+            gu = jnp.dot(x[pl.ds(at, part), :], w[...], preferred_element_type=jnp.float32) * scale
             for j in range(part // blk):
                 gate = gu[j * blk:(j + 1) * blk, :uw]
                 up = gu[j * blk:(j + 1) * blk, uw:]
-                upstream = hg[meta[1 + i * (part // blk) + j]].astype(jnp.float32)
+                upstream = hg[meta[1 + (i % 2) * (part // blk) + j], pl.ds(half, blk), :].astype(jnp.float32)
                 sigma = jax.nn.sigmoid(gate)
                 g = upstream * up * sigma * (1.0 + gate * (1.0 - sigma))
                 u = upstream * gate * sigma
@@ -139,11 +179,11 @@
         def band(i, carry):
             at = pl.multiple_of(i * part, part)
             grad = lax.dot_general(x[:, pl.ds(at, part)], rows[...], (((0,), (0,)), ((), ())), preferred_element_type=jnp.float32)
-            old = w[0, pl.ds(at, part), :].astype(jnp.float32)
+            old = w[pl.ds(at, part), :].astype(jnp.float32)
             out[pl.ds(at, part), :] = (old - 0.5 * (grad * scale)).astype(jnp.bfloat16)
             return carry
 
-        lax.fori_loop(0, w.shape[1] // part, band, 0)
+        lax.fori_loop(0, w.shape[0] // part, band, 0)
 
     if other is not None:
         @pl.when(meta[0] != which)
@@ -156,20 +196,17 @@
     n = sum(v.shape[0] for v in xs)
     both = w.shape[2]
     return pl.pallas_call(
-        functools.partial(step_body, which, len(xs)),
+        functools.partial(step_body, which, len(xs), c),
         grid=(1,),
         out_shape=jax.ShapeDtypeStruct((width, both), jnp.bfloat16),
-        in_specs=[
-            SMEM,
-            pl.BlockSpec(hg.shape[:2] + (both // 2,), lambda i: (0, 0, c)),
-            pl.BlockSpec((1, width, both), lambda i: (c, 0, 0)),
-        ]
-        + [HBM] * (len(xs) + len(extra)),
+        in_specs=[SMEM] + [HBM] * (2 + len(xs) + len(extra)),
         out_specs=pl.BlockSpec((width, both), lambda i: (0, 0)),
         scratch_shapes=[
             pltpu.VMEM((n, width), jnp.bfloat16),
+            pltpu.VMEM((width, both), jnp.bfloat16),
+            pltpu.VMEM(hg.shape[:2] + (both // 2,), jnp.bfloat16),
             pltpu.VMEM((n, both), jnp.bfloat16),
-            pltpu.SemaphoreType.DMA((n // 512,)),
+            pltpu.SemaphoreType.DMA((n // 512 + 2,)),
         ],
         compiler_params=params(32),
         cost_estimate=pl.CostEstimate(flops=4 * n * width * both, bytes_accessed=n * width * 2, transcendentals=n * 128),
@@ -227,8 +264,11 @@
     def send(v, move):
         return lax.ppermute(v, axes, device_pairs(groups, move))
 
-    def along_x(v, which, by):
-        return send(v, lambda g, u, t: (g, u, t + by) if g % 2 == which else None)
+    def along_x(v, by):
+        return send(v, lambda g, u, t: (g, u, t + by))
+
+    def along_z(v, by):
+        return send(v, lambda g, u, t: (g, u + by, t))
 
     def table(pairs):
         up = jnp.array([k for k, d in pairs], jnp.int32)
@@ -236,41 +276,41 @@
         src = ((z + NZ - up) % NZ) * NX + (x + NX - along) % NX
         return jnp.concatenate([core.reshape(1), src]).astype(jnp.int32)
 
-    halves = ((0, 1), (2, 3))
-    meta_a = table([(k, d) for h in halves for d in DX for k in h])
+    meta_a = table([(k, d) for k in range(NZ) for d in DX])
     meta_b = table([(k, d) for d in DX for k in range(NZ)])
 
-    def ahead_by(v):
-        return send(v, lambda g, u, t: (g, u + 1, t))
-
-    def fan(v, which):
+    def fan(v):
         out = [v]
         for d in DX[1:]:
-            out.append(along_x(v, which, d))
+            out.append(along_x(v, d))
         return out
 
     def swap(v):
         return send(v, lambda g, u, t: (g + 1 - 2 * (g % 2), u, t))
 
+    half_a, half_b = pick(meta_a, own, swap(own))
     w = pack_weights(w_gate[0], w_up[0])
-    r1 = ahead_by(own)
-    r2 = ahead_by(r1)
-    first = cat([own, r1])
-    ahead = fan(first, 0)
-    r3 = ahead_by(r2)
-    hg = split_units(hidden_grad[0], NZ * NX, r2)
+    r1 = along_z(half_a, 1)
+    own_a = fan(half_a)
+    r2 = along_z(r1, 1)
+    one_a = fan(r1)
+    r3 = along_z(r2, 1)
+    two_a = fan(r2)
+    hg = split_units(hidden_grad[0], NZ * NX)
     hg = lax.all_to_all(hg, "dp", split_axis=0, concat_axis=0, tiled=True)
-    second = cat([r2, r3])
-    behind = fan(second, 0)
+    three_a = fan(r3)
+    column_b = [along_z(half_b, k) for k in range(1, NZ)]
+    early = cat(own_a + one_a + two_a)
+    late = cat(three_a)
+    pieces = [early, late, swap(early), swap(late)]
 
     step_a, cross_a = [], []
     for c in range(CHUNKS):
-        step_a.append(step_chunk(0, c, meta_a, hg, w, ahead + behind))
+        step_a.append(step_chunk(0, c, meta_a, hg, w, pieces))
         cross_a.append(send(step_a[c], lambda g, u, t: (g - 1, u, t) if g % 2 == 0 else None))
 
-    token = swap(step_a[0][:8, :128])
-    block = cat([first, second], token, *step_a)
-    blocks = fan(block, 1)
+    blocks = cat(fan(cat([half_b] + column_b, step_a[0])))
+    blocks = [blocks, swap(blocks)]
     mine, cross_b, near = [], [], []
     for c in range(CHUNKS):
         mine.append(step_chunk(1, c, meta_b, hg, w, blocks, step_a[c]))

time: 289 us -> 344 us (1.19)
  waiting for transfers between devices: 132 us -> 229 us
  starting transfers between devices: 105 us -> 64.9 us
    ppermute x22 -> x34, waiting for transfers between devices: 132 us -> 229 us  [send(): return lax.ppermute(v, axes, device_pairs(groups, move))]
    ppermute x22 -> x34, starting transfers between devices: 97.3 us -> 56.1 us  [send(): return lax.ppermute(v, axes, device_pairs(groups, move))]
    pallas_call x6 -> x7, Pallas kernels: 29.2 us -> 26.5 us  [the longest x6 25.9 us: step_chunk(): pl.pallas_call(functools.partial(step_body, which, len(xs), c), grid=(1,)...]
    unnamed x24 -> x30, local copies, waits for them, and re-layouts: 8.72 us -> 9.81 us
  transfers between devices with their start and end apart: 23 -> 35, of which waited for: 8 -> 18; matrix products, arithmetic and copies ran while one was open for 0% -> 0% of each run, Pallas kernels for 9% -> 10%
where the time goes in v2:
time: 344 us; the launch traced here: 343 us
  waiting for transfers between devices  229 us (67%)
  starting transfers between devices  64.9 us (19%)
  Pallas kernels  38.1 us (11%)
  local copies, waits for them, and re-layouts  9.81 us (3%)
    ppermute x34, waiting for transfers between devices, send(): return lax.ppermute(v, axes, device_pairs(groups, move))  229 us
    ppermute x34, starting transfers between devices, send(): return lax.ppermute(v, axes, device_pairs(groups, move))  56.1 us
    pallas_call x6, Pallas kernels, step_chunk(): pl.pallas_call(functools.partial(step_body, which, len(xs), c), grid=(1,)...  25.9 us
    unnamed x30, local copies, waits for them, and re-layouts  9.81 us
    all_to_all x1, starting transfers between devices, local(): hg = lax.all_to_all(hg, 'dp', split_axis=0, concat_axis=0, tiled=True)  8.8 us
    pallas_call x3, Pallas kernels, mix_chunk(): pl.pallas_call(mix_body, grid=(width // band,), out_shape=(jax.ShapeDtype...  7.28 us
  transfers between devices with their start and end apart: 35, of which 18 were waited for; matrix products, arithmetic and copies ran while one was open for 0% of the time, Pallas kernels for 10%

profile of v2, /device:TPU:38, one launch (start us, length us, event | category | flops | bytes accessed | tf_op | source)
XLA Modules:
  0.0 343.4 jit_solution(5343505802024211479)
XLA Ops:
  0.8 0.7 fusion
  1.5 1.3 collective-permute-done.got
  2.8 1.0 copy-done.8
  3.9 0.6 pick.1
  4.5 2.0 collective-permute-start.7
  6.5 1.4 collective-permute-start.6
  7.9 5.0 %collective-permute-done.7.refs_4_ = bf16[64,2048]{1,0:T(8,128)(2,1)S(1)} collective-permute-done((bf16[64,2048]{1,0:T(8,128)(2,1)S(1)}, bf16[64,2048]{1,0:T(8,128)(2,1)S(1)}, u32[]{:S(2)}, u32[]{:S(2)}) %collective-permute-start.7) | collective-permute-done | bytes 262176 | tf_op jit(solution)/shard_map/ppermute | solution.py:265
  12.9 1.9 collective-permute-start.11
  14.9 0.5 collective-permute-start.4
  15.3 2.4 collective-permute-start.10
  17.8 5.2 %collective-permute-done.5.refs_2_ = bf16[64,2048]{1,0:T(8,128)(2,1)S(1)} collective-permute-done((bf16[64,2048]{1,0:T(8,128)(2,1)S(1)}, bf16[64,2048]{1,0:T(8,128)(2,1)S(1)}, u32[]{:S(2)}, u32[]{:S(2)}) %collective-permute-start.5) | collective-permute-done | bytes 262176 | tf_op jit(solution)/shard_map/ppermute | solution.py:265
  22.9 0.5 collective-permute-start.8
  23.4 1.4 collective-permute-start.14
  24.8 0.9 collective-permute-start.13
  25.7 2.8 collective-permute-done.10.refs_7_
  28.5 3.8 %collective-permute-start.12 = (bf16[64,2048]{1,0:T(8,128)(2,1)S(1)}, bf16[64,2048]{1,0:T(8,128)(2,1)S(1)}, u32[]{:S(2)}, u32[]{:S(2)}) collective-permute-start(bf16[64,2048]{1,0:T(8,128)(2,1)S(1)} %collective-permute-done.11.refs_8_), channel_id=1, source_target_pairs={{0,1},{1,2},{2,3},{3,0},{4,5},{5,6},{6,7},{7,4},{8,9},{9,10},{10,1... | collective-permute-start | bytes 786440 | tf_op jit(solution)/shard_map/ppermute | solution.py:265
  32.3 1.8 collective-permute-done.9.refs_6_
  34.1 1.1 collective-permute-done.8.refs_5_
  35.3 4.5 %collective-permute-done.14.refs_11_ = bf16[64,2048]{1,0:T(8,128)(2,1)S(1)} collective-permute-done((bf16[64,2048]{1,0:T(8,128)(2,1)S(1)}, bf16[64,2048]{1,0:T(8,128)(2,1)S(1)}, u32[]{:S(2)}, u32[]{:S(2)}) %collective-permute-start.14) | collective-permute-done | bytes 262176 | tf_op jit(solution)/shard_map/ppermute | solution.py:265
  39.8 4.4 %collective-permute-done.13.refs_10_ = bf16[64,2048]{1,0:T(8,128)(2,1)S(1)} collective-permute-done((bf16[64,2048]{1,0:T(8,128)(2,1)S(1)}, bf16[64,2048]{1,0:T(8,128)(2,1)S(1)}, u32[]{:S(2)}, u32[]{:S(2)}) %collective-permute-start.13) | collective-permute-done | bytes 262176 | tf_op jit(solution)/shard_map/ppermute | solution.py:265
  44.2 0.4 collective-permute-done.12.refs_9_
  44.6 0.3 cat.4.refs_0_
  45.1 1.3 split.1
  46.3 8.8 %all-to-all-start = ((bf16[16,128,384]{2,1,0:T(8,128)(2,1)}), bf16[16,128,384]{2,1,0:T(8,128)(2,1)}, u32[]{:S(2)}, u32[]{:S(2)}) async-start(bf16[16,128,384]{2,1,0:T(8,128)(2,1)} %split.1), calls=%async_computation | async-start | bytes 3145728 | tf_op jit(solution)/shard_map/all_to_all | solution.py:300
  55.1 1.5 collective-permute-start.15
  56.7 38.5 %collective-permute-done.15.refs_0_ = bf16[64,2048]{1,0:T(8,128)(2,1)S(1)} collective-permute-done((bf16[64,2048]{1,0:T(8,128)(2,1)}, bf16[64,2048]{1,0:T(8,128)(2,1)S(1)}, u32[]{:S(2)}, u32[]{:S(2)}) %collective-permute-start.15) | collective-permute-done | bytes 262176 | tf_op jit(solution)/shard_map/ppermute | solution.py:265
  95.2 1.5 collective-permute-start.18
  96.6 3.2 collective-permute-start.16
  99.9 6.0 %collective-permute-done.18.refs_3_ = bf16[64,2048]{1,0:T(8,128)(2,1)S(1)} collective-permute-done((bf16[64,2048]{1,0:T(8,128)(2,1)S(1)}, bf16[64,2048]{1,0:T(8,128)(2,1)S(1)}, u32[]{:S(2)}, u32[]{:S(2)}) %collective-permute-start.18) | collective-permute-done | bytes 262176 | tf_op jit(solution)/shard_map/ppermute | solution.py:265
  105.9 4.0 %collective-permute-done.17.refs_2_ = bf16[64,2048]{1,0:T(8,128)(2,1)S(1)} collective-permute-done((bf16[64,2048]{1,0:T(8,128)(2,1)S(1)}, bf16[64,2048]{1,0:T(8,128)(2,1)S(1)}, u32[]{:S(2)}, u32[]{:S(2)}) %collective-permute-start.17) | collective-permute-done | bytes 262176 | tf_op jit(solution)/shard_map/ppermute | solution.py:265
  110.1 1.7 copy-done.4
  111.8 1.2 pack.1.packed
  113.0 1.7 copy-done
  114.6 3.8 %collective-permute-start.2 = (bf16[64,2048]{1,0:T(8,128)(2,1)S(1)}, bf16[64,2048]{1,0:T(8,128)(2,1)}, u32[]{:S(2)}, u32[]{:S(2)}) collective-permute-start(bf16[64,2048]{1,0:T(8,128)(2,1)S(1)} %get-tuple-element.10.refs_0_), channel_id=1, source_target_pairs={{0,8},{1,9},{2,10},{3,11},{4,12},{5,13},{6,14},{7,15},{8,0},{9,1},... | collective-permute-start | bytes 786440 | tf_op jit(solution)/shard_map/ppermute | solution.py:265
  118.5 1.1 copy-done.10
  119.5 1.9 copy-done.1
  121.4 1.2 copy-done.6
  122.6 1.2 copy-done.11
  123.9 7.9 %step.6.refs_4_.refs_2_ = bf16[2048,256]{1,0:T(8,128)(2,1)S(1)} custom-call(s32[17]{0:T(128)S(1)} %pad_add_fusion.meta, bf16[16,128,384]{2,1,0:T(8,128)(2,1)} %all-to-all-done.units, bf16[3,2048,256]{2,1,0:T(8,128)(2,1)S(1)} %copy-done.1, bf16[768,2048]{1,0:T(8,128)(2,1)S(1)} %cat.4.refs_0_, bf16[256,2048]{1,0:T(8,128)(2,1)S(1)} %copy-done.6, ...), custom_call_target="tpu_custom_call" | custom-call | flops 4294967296 | bytes 8388608 | tf_op jit(solution)/shard_map/step/pallas_call | solution.py:198
  131.8 3.3 collective-permute-done.1.refs_1_
  135.1 1.2 cat.6.refs_0_
  136.3 1.6 collective-permute-start.23
  138.0 3.1 collective-permute-start.21
  141.1 22.8 %collective-permute-done.23.refs_3_ = bf16[256,2048]{1,0:T(8,128)(2,1)S(1)} collective-permute-done((bf16[256,2048]{1,0:T(8,128)(2,1)S(1)}, bf16[256,2048]{1,0:T(8,128)(2,1)S(1)}, u32[]{:S(2)}, u32[]{:S(2)}) %collective-permute-start.23) | collective-permute-done | bytes 1048608 | tf_op jit(solution)/shard_map/ppermute | solution.py:265
  163.9 21.5 %collective-permute-done.22.refs_2_ = bf16[256,2048]{1,0:T(8,128)(2,1)S(1)} collective-permute-done((bf16[256,2048]{1,0:T(8,128)(2,1)S(1)}, bf16[256,2048]{1,0:T(8,128)(2,1)S(1)}, u32[]{:S(2)}, u32[]{:S(2)}) %collective-permute-start.22) | collective-permute-done | bytes 1048608 | tf_op jit(solution)/shard_map/ppermute | solution.py:265
  185.4 0.3 cat.7.refs_0_
  186.0 10.3 %collective-permute-start.32 = (bf16[2048,256]{1,0:T(8,128)(2,1)S(1)}, bf16[2048,256]{1,0:T(8,128)(2,1)S(1)}, u32[]{:S(2)}, u32[]{:S(2)}) collective-permute-start(bf16[2048,256]{1,0:T(8,128)(2,1)S(1)} %step.6.refs_4_.refs_2_), channel_id=1, source_target_pairs={{0,240},{1,241},{2,242},{3,243},{4,244},{5,245},{6,246},{7,247},{8... | collective-permute-start | bytes 3145736 | tf_op jit(solution)/shard_map/ppermute | solution.py:265
  196.3 7.9 %step.9.refs_2_ = bf16[2048,256]{1,0:T(8,128)(2,1)S(1)} custom-call(s32[17]{0:T(128)S(1)} %pad_add_fusion.meta, bf16[16,128,384]{2,1,0:T(8,128)(2,1)} %all-to-all-done.units, bf16[3,2048,256]{2,1,0:T(8,128)(2,1)S(1)} %copy-done.1, bf16[768,2048]{1,0:T(8,128)(2,1)S(1)} %cat.4.refs_0_, bf16[256,2048]{1,0:T(8,128)(2,1)S(1)} %copy-done.6, ...), custom_call_target="tpu_custom_call" | custom-call | flops 4294967296 | bytes 8388608 | tf_op jit(solution)/shard_map/step/pallas_call | solution.py:198
  204.2 1.5 collective-permute-start.29
  205.7 0.7 step.11.own
  206.4 1.3 collective-permute-start.33
  207.8 8.1 %step.7.refs_2_ = bf16[2048,256]{1,0:T(8,128)(2,1)S(1)} custom-call(s32[17]{0:T(128)S(1)} %pad_add_fusion.meta, bf16[16,128,384]{2,1,0:T(8,128)(2,1)} %all-to-all-done.units, bf16[3,2048,256]{2,1,0:T(8,128)(2,1)S(1)} %copy-done.1, bf16[768,2048]{1,0:T(8,128)(2,1)S(1)} %cat.4.refs_0_, bf16[256,2048]{1,0:T(8,128)(2,1)S(1)} %copy-done.7, ...), custom_call_target="tpu_custom_call" | custom-call | flops 4294967296 | bytes 8388608 | tf_op jit(solution)/shard_map/step/pallas_call | solution.py:198
  215.9 0.7 step.10.own
  216.6 1.3 collective-permute-start.30
  217.9 0.7 step.8.own
  218.6 88.0 %collective-permute-done.29.far_a = bf16[2048,256]{1,0:T(8,128)(2,1)S(1)} collective-permute-done((bf16[2048,256]{1,0:T(8,128)(2,1)S(1)}, bf16[2048,256]{1,0:T(8,128)(2,1)S(1)}, u32[]{:S(2)}, u32[]{:S(2)}) %collective-permute-start.29) | collective-permute-done | bytes 1048608 | tf_op jit(solution)/shard_map/ppermute | solution.py:265
  306.6 1.0 collective-permute-start.28
  307.6 9.0 %collective-permute-start.26 = (bf16[2048,256]{1,0:T(8,128)(2,1)S(1)}, bf16[2048,256]{1,0:T(8,128)(2,1)S(1)}, u32[]{:S(2)}, u32[]{:S(2)}) collective-permute-start(bf16[2048,256]{1,0:T(8,128)(2,1)S(1)} %step.7.refs_2_), channel_id=1, source_target_pairs={{0,240},{1,241},{2,242},{3,243},{4,244},{5,245},{6,246},{7,247},{8... | collective-permute-start | bytes 3145736 | tf_op jit(solution)/shard_map/ppermute | solution.py:265
  316.6 1.3 collective-permute-start.27
  318.1 2.4 mix.3
  320.5 2.4 mix.4
  322.9 17.1 %collective-permute-done.26.far_a = bf16[2048,256]{1,0:T(8,128)(2,1)S(1)} collective-permute-done((bf16[2048,256]{1,0:T(8,128)(2,1)S(1)}, bf16[2048,256]{1,0:T(8,128)(2,1)S(1)}, u32[]{:S(2)}, u32[]{:S(2)}) %collective-permute-start.26) | collective-permute-done | bytes 1048608 | tf_op jit(solution)/shard_map/ppermute | solution.py:265
  340.0 1.0 collective-permute-done.27.far_b
  341.0 2.4 mix.5
  (56 shorter events, 1.1 us)
Async XLA Ops:
  0.6 2.2 collective-permute-start
  2.8 1.0 copy-start.8
  4.5 40.6 %copy-start.2 = (bf16[1,128,6144]{2,1,0:T(8,128)(2,1)S(1)}, bf16[1,128,6144]{2,1,0:T(8,128)(2,1)}, u32[]{:S(2)}) copy-start(bf16[1,128,6144]{2,1,0:T(8,128)(2,1)} %param.9) | copy-start | bytes 4718596
  4.5 8.4 %collective-permute-start.7 = (bf16[64,2048]{1,0:T(8,128)(2,1)S(1)}, bf16[64,2048]{1,0:T(8,128)(2,1)S(1)}, u32[]{:S(2)}, u32[]{:S(2)}) collective-permute-start(bf16[64,2048]{1,0:T(8,128)(2,1)S(1)} %get-tuple-element.11.refs_0_), channel_id=1, source_target_pairs={{0,4},{1,5},{2,6},{3,7},{4,8},{5,9},{6,10},{7,11},{8,12},{9,13},{1... | collective-permute-start | bytes 786440 | tf_op jit(solution)/shard_map/ppermute | solution.py:265
  6.5 11.2 %collective-permute-start.6 = (bf16[64,2048]{1,0:T(8,128)(2,1)S(1)}, bf16[64,2048]{1,0:T(8,128)(2,1)S(1)}, u32[]{:S(2)}, u32[]{:S(2)}) collective-permute-start(bf16[64,2048]{1,0:T(8,128)(2,1)S(1)} %get-tuple-element.11.refs_0_), channel_id=1, source_target_pairs={{0,2},{1,3},{2,0},{3,1},{4,6},{5,7},{6,4},{7,5},{8,10},{9,11},{10,... | collective-permute-start | bytes 786440 | tf_op jit(solution)/shard_map/ppermute | solution.py:265
  7.9 15.0 %collective-permute-start.5 = (bf16[64,2048]{1,0:T(8,128)(2,1)S(1)}, bf16[64,2048]{1,0:T(8,128)(2,1)S(1)}, u32[]{:S(2)}, u32[]{:S(2)}) collective-permute-start(bf16[64,2048]{1,0:T(8,128)(2,1)S(1)} %get-tuple-element.11.refs_0_), channel_id=1, source_target_pairs={{0,3},{1,0},{2,1},{3,2},{4,7},{5,4},{6,5},{7,6},{8,11},{9,8},{10,9... | collective-permute-start | bytes 786440 | tf_op jit(solution)/shard_map/ppermute | solution.py:265
  12.9 10.5 %collective-permute-start.11 = (bf16[64,2048]{1,0:T(8,128)(2,1)S(1)}, bf16[64,2048]{1,0:T(8,128)(2,1)S(1)}, u32[]{:S(2)}, u32[]{:S(2)}) collective-permute-start(bf16[64,2048]{1,0:T(8,128)(2,1)S(1)} %collective-permute-done.7.refs_4_), channel_id=1, source_target_pairs={{0,4},{1,5},{2,6},{3,7},{4,8},{5,9},{6,10},{7,11},{8,12},{9,13},{1... | collective-permute-start | bytes 786440 | tf_op jit(solution)/shard_map/ppermute | solution.py:265
  14.9 10.0 %collective-permute-start.4 = (bf16[64,2048]{1,0:T(8,128)(2,1)S(1)}, bf16[64,2048]{1,0:T(8,128)(2,1)S(1)}, u32[]{:S(2)}, u32[]{:S(2)}) collective-permute-start(bf16[64,2048]{1,0:T(8,128)(2,1)S(1)} %get-tuple-element.11.refs_0_), channel_id=1, source_target_pairs={{0,1},{1,2},{2,3},{3,0},{4,5},{5,6},{6,7},{7,4},{8,9},{9,10},{10,1... | collective-permute-start | bytes 786440 | tf_op jit(solution)/shard_map/ppermute | solution.py:265
  15.3 13.2 %collective-permute-start.10 = (bf16[64,2048]{1,0:T(8,128)(2,1)S(1)}, bf16[64,2048]{1,0:T(8,128)(2,1)S(1)}, u32[]{:S(2)}, u32[]{:S(2)}) collective-permute-start(bf16[64,2048]{1,0:T(8,128)(2,1)S(1)} %collective-permute-done.7.refs_4_), channel_id=1, source_target_pairs={{0,2},{1,3},{2,0},{3,1},{4,6},{5,7},{6,4},{7,5},{8,10},{9,11},{10,... | collective-permute-start | bytes 786440 | tf_op jit(solution)/shard_map/ppermute | solution.py:265
  17.8 16.4 %collective-permute-start.9 = (bf16[64,2048]{1,0:T(8,128)(2,1)S(1)}, bf16[64,2048]{1,0:T(8,128)(2,1)S(1)}, u32[]{:S(2)}, u32[]{:S(2)}) collective-permute-start(bf16[64,2048]{1,0:T(8,128)(2,1)S(1)} %collective-permute-done.7.refs_4_), channel_id=1, source_target_pairs={{0,3},{1,0},{2,1},{3,2},{4,7},{5,4},{6,5},{7,6},{8,11},{9,8},{10,9... | collective-permute-start | bytes 786440 | tf_op jit(solution)/shard_map/ppermute | solution.py:265
  22.9 12.4 %collective-permute-start.8 = (bf16[64,2048]{1,0:T(8,128)(2,1)S(1)}, bf16[64,2048]{1,0:T(8,128)(2,1)S(1)}, u32[]{:S(2)}, u32[]{:S(2)}) collective-permute-start(bf16[64,2048]{1,0:T(8,128)(2,1)S(1)} %collective-permute-done.7.refs_4_), channel_id=1, source_target_pairs={{0,1},{1,2},{2,3},{3,0},{4,5},{5,6},{6,7},{7,4},{8,9},{9,10},{10,1... | collective-permute-start | bytes 786440 | tf_op jit(solution)/shard_map/ppermute | solution.py:265
  23.4 21.5 %copy-start.9 = (bf16[64,2048]{1,0:T(8,128)(2,1)}, bf16[64,2048]{1,0:T(8,128)(2,1)S(1)}, u32[]{:S(2)}) copy-start(bf16[64,2048]{1,0:T(8,128)(2,1)S(1)} %collective-permute-done.11.refs_8_) | copy-start | bytes 786436
  23.4 16.4 %collective-permute-start.14 = (bf16[64,2048]{1,0:T(8,128)(2,1)S(1)}, bf16[64,2048]{1,0:T(8,128)(2,1)S(1)}, u32[]{:S(2)}, u32[]{:S(2)}) collective-permute-start(bf16[64,2048]{1,0:T(8,128)(2,1)S(1)} %collective-permute-done.11.refs_8_), channel_id=1, source_target_pairs={{0,2},{1,3},{2,0},{3,1},{4,6},{5,7},{6,4},{7,5},{8,10},{9,11},{10,... | collective-permute-start | bytes 786440 | tf_op jit(solution)/shard_map/ppermute | solution.py:265
  24.8 19.3 %collective-permute-start.13 = (bf16[64,2048]{1,0:T(8,128)(2,1)S(1)}, bf16[64,2048]{1,0:T(8,128)(2,1)S(1)}, u32[]{:S(2)}, u32[]{:S(2)}) collective-permute-start(bf16[64,2048]{1,0:T(8,128)(2,1)S(1)} %collective-permute-done.11.refs_8_), channel_id=1, source_target_pairs={{0,3},{1,0},{2,1},{3,2},{4,7},{5,4},{6,5},{7,6},{8,11},{9,8},{10,9... | collective-permute-start | bytes 786440 | tf_op jit(solution)/shard_map/ppermute | solution.py:265
  28.5 16.1 %collective-permute-start.12 = (bf16[64,2048]{1,0:T(8,128)(2,1)S(1)}, bf16[64,2048]{1,0:T(8,128)(2,1)S(1)}, u32[]{:S(2)}, u32[]{:S(2)}) collective-permute-start(bf16[64,2048]{1,0:T(8,128)(2,1)S(1)} %collective-permute-done.11.refs_8_), channel_id=1, source_target_pairs={{0,1},{1,2},{2,3},{3,0},{4,5},{5,6},{6,7},{7,4},{8,9},{9,10},{10,1... | collective-permute-start | bytes 786440 | tf_op jit(solution)/shard_map/ppermute | solution.py:265
  45.0 74.6 %collective-permute-start.19 = (bf16[768,2048]{1,0:T(8,128)(2,1)S(1)}, bf16[768,2048]{1,0:T(8,128)(2,1)}, u32[]{:S(2)}, u32[]{:S(2)}) collective-permute-start(bf16[768,2048]{1,0:T(8,128)(2,1)S(1)} %cat.4.refs_0_), channel_id=1, source_target_pairs={{0,16},{1,17},{2,18},{3,19},{4,20},{5,21},{6,22},{7,23},{8,24},{9,... | collective-permute-start | bytes 9437192 | tf_op jit(solution)/shard_map/ppermute | solution.py:265
  46.3 73.2 %all-to-all-start = ((bf16[16,128,384]{2,1,0:T(8,128)(2,1)}), bf16[16,128,384]{2,1,0:T(8,128)(2,1)}, u32[]{:S(2)}, u32[]{:S(2)}) async-start(bf16[16,128,384]{2,1,0:T(8,128)(2,1)} %split.1), calls=%async_computation | async-start | bytes 3145728 | tf_op jit(solution)/shard_map/all_to_all | solution.py:300
  55.1 55.0 %copy-start.3 = (bf16[1,2048,384]{2,1,0:T(8,128)(2,1)S(1)}, bf16[1,2048,384]{2,1,0:T(8,128)(2,1)}, u32[]{:S(2)}) copy-start(bf16[1,2048,384]{2,1,0:T(8,128)(2,1)} %param.10) | copy-start | bytes 4718596
  55.1 40.0 %collective-permute-start.15 = (bf16[64,2048]{1,0:T(8,128)(2,1)}, bf16[64,2048]{1,0:T(8,128)(2,1)S(1)}, u32[]{:S(2)}, u32[]{:S(2)}) collective-permute-start(bf16[64,2048]{1,0:T(8,128)(2,1)} %copy-done.9), channel_id=1, source_target_pairs={{0,4},{1,5},{2,6},{3,7},{4,8},{5,9},{6,10},{7,11},{8,12},{9,13},{1... | collective-permute-start | bytes 786440 | tf_op jit(solution)/shard_map/ppermute | solution.py:265
  95.2 10.7 %collective-permute-start.18 = (bf16[64,2048]{1,0:T(8,128)(2,1)S(1)}, bf16[64,2048]{1,0:T(8,128)(2,1)S(1)}, u32[]{:S(2)}, u32[]{:S(2)}) collective-permute-start(bf16[64,2048]{1,0:T(8,128)(2,1)S(1)} %collective-permute-done.15.refs_0_), channel_id=1, source_target_pairs={{0,2},{1,3},{2,0},{3,1},{4,6},{5,7},{6,4},{7,5},{8,10},{9,11},{10,... | collective-permute-start | bytes 786440 | tf_op jit(solution)/shard_map/ppermute | solution.py:265
  96.6 13.2 %collective-permute-start.17 = (bf16[64,2048]{1,0:T(8,128)(2,1)S(1)}, bf16[64,2048]{1,0:T(8,128)(2,1)S(1)}, u32[]{:S(2)}, u32[]{:S(2)}) collective-permute-start(bf16[64,2048]{1,0:T(8,128)(2,1)S(1)} %collective-permute-done.15.refs_0_), channel_id=1, source_target_pairs={{0,3},{1,0},{2,1},{3,2},{4,7},{5,4},{6,5},{7,6},{8,11},{9,8},{10,9... | collective-permute-start | bytes 786440 | tf_op jit(solution)/shard_map/ppermute | solution.py:265
  96.6 13.2 %collective-permute-start.16 = (bf16[64,2048]{1,0:T(8,128)(2,1)S(1)}, bf16[64,2048]{1,0:T(8,128)(2,1)S(1)}, u32[]{:S(2)}, u32[]{:S(2)}) collective-permute-start(bf16[64,2048]{1,0:T(8,128)(2,1)S(1)} %collective-permute-done.15.refs_0_), channel_id=1, source_target_pairs={{0,1},{1,2},{2,3},{3,0},{4,5},{5,6},{6,7},{7,4},{8,9},{9,10},{10,1... | collective-permute-start | bytes 786440 | tf_op jit(solution)/shard_map/ppermute | solution.py:265
  110.0 3.0 copy-start.5
  110.0 8.5 %collective-permute-start.20 = (bf16[256,2048]{1,0:T(8,128)(2,1)S(1)}, bf16[256,2048]{1,0:T(8,128)(2,1)S(1)}, u32[]{:S(2)}, u32[]{:S(2)}) collective-permute-start(bf16[256,2048]{1,0:T(8,128)(2,1)S(1)} %cat.5.refs_1_), channel_id=1, source_target_pairs={{0,16},{1,17},{2,18},{3,19},{4,20},{5,21},{6,22},{7,23},{8,24},{9,... | collective-permute-start | bytes 3145736 | tf_op jit(solution)/shard_map/ppermute | solution.py:265
  110.1 1.7 copy-start.4
  112.9 1.7 copy-start
  114.6 17.1 %collective-permute-start.3 = (bf16[64,2048]{1,0:T(8,128)(2,1)S(1)}, bf16[64,2048]{1,0:T(8,128)(2,1)}, u32[]{:S(2)}, u32[]{:S(2)}) collective-permute-start(bf16[64,2048]{1,0:T(8,128)(2,1)S(1)} %get-tuple-element.10.refs_0_), channel_id=1, source_target_pairs={{0,12},{1,13},{2,14},{3,15},{4,0},{5,1},{6,2},{7,3},{8,4},{9,5},{1... | collective-permute-start | bytes 786440 | tf_op jit(solution)/shard_map/ppermute | solution.py:265
  114.6 17.1 %collective-permute-start.2 = (bf16[64,2048]{1,0:T(8,128)(2,1)S(1)}, bf16[64,2048]{1,0:T(8,128)(2,1)}, u32[]{:S(2)}, u32[]{:S(2)}) collective-permute-start(bf16[64,2048]{1,0:T(8,128)(2,1)S(1)} %get-tuple-element.10.refs_0_), channel_id=1, source_target_pairs={{0,8},{1,9},{2,10},{3,11},{4,12},{5,13},{6,14},{7,15},{8,0},{9,1},... | collective-permute-start | bytes 786440 | tf_op jit(solution)/shard_map/ppermute | solution.py:265
  118.5 16.6 %collective-permute-start.1 = (bf16[64,2048]{1,0:T(8,128)(2,1)S(1)}, bf16[64,2048]{1,0:T(8,128)(2,1)}, u32[]{:S(2)}, u32[]{:S(2)}) collective-permute-start(bf16[64,2048]{1,0:T(8,128)(2,1)S(1)} %get-tuple-element.10.refs_0_), channel_id=1, source_target_pairs={{0,4},{1,5},{2,6},{3,7},{4,8},{5,9},{6,10},{7,11},{8,12},{9,13},{1... | collective-permute-start | bytes 786440 | tf_op jit(solution)/shard_map/ppermute | solution.py:265
  118.5 1.1 copy-start.10
  119.5 1.9 copy-start.1
  121.4 1.2 copy-start.6
  122.6 1.2 copy-start.11
  136.2 49.6 %copy-start.13 = (s32[16]{0:T(128)S(1)}, s32[16]{0:T(128)}, u32[]{:S(2)}) copy-start(s32[16]{0:T(128)} %constant.84) | copy-start | bytes 196
  136.3 49.6 %copy-start.14 = (s32[16]{0:T(128)S(1)}, s32[16]{0:T(128)}, u32[]{:S(2)}) copy-start(s32[16]{0:T(128)} %constant.83) | copy-start | bytes 196
  136.3 60.0 %copy-start.12 = (bf16[256,2048]{1,0:T(8,128)(2,1)S(1)}, bf16[256,2048]{1,0:T(8,128)(2,1)}, u32[]{:S(2)}) copy-start(bf16[256,2048]{1,0:T(8,128)(2,1)} %copy-done.10) | copy-start | bytes 3145732
  136.3 27.7 %collective-permute-start.23 = (bf16[256,2048]{1,0:T(8,128)(2,1)S(1)}, bf16[256,2048]{1,0:T(8,128)(2,1)S(1)}, u32[]{:S(2)}, u32[]{:S(2)}) collective-permute-start(bf16[256,2048]{1,0:T(8,128)(2,1)S(1)} %cat.6.refs_0_), channel_id=1, source_target_pairs={{0,2},{1,3},{2,0},{3,1},{4,6},{5,7},{6,4},{7,5},{8,10},{9,11},{10,... | collective-permute-start | bytes 3145736 | tf_op jit(solution)/shard_map/ppermute | solution.py:265
  137.9 47.6 %collective-permute-start.22 = (bf16[256,2048]{1,0:T(8,128)(2,1)S(1)}, bf16[256,2048]{1,0:T(8,128)(2,1)S(1)}, u32[]{:S(2)}, u32[]{:S(2)}) collective-permute-start(bf16[256,2048]{1,0:T(8,128)(2,1)S(1)} %cat.6.refs_0_), channel_id=1, source_target_pairs={{0,3},{1,0},{2,1},{3,2},{4,7},{5,4},{6,5},{7,6},{8,11},{9,8},{10,9... | collective-permute-start | bytes 3145736 | tf_op jit(solution)/shard_map/ppermute | solution.py:265
  138.0 47.4 %collective-permute-start.21 = (bf16[256,2048]{1,0:T(8,128)(2,1)S(1)}, bf16[256,2048]{1,0:T(8,128)(2,1)S(1)}, u32[]{:S(2)}, u32[]{:S(2)}) collective-permute-start(bf16[256,2048]{1,0:T(8,128)(2,1)S(1)} %cat.6.refs_0_), channel_id=1, source_target_pairs={{0,1},{1,2},{2,3},{3,0},{4,5},{5,6},{6,7},{7,4},{8,9},{9,10},{10,1... | collective-permute-start | bytes 3145736 | tf_op jit(solution)/shard_map/ppermute | solution.py:265
  185.8 19.9 %collective-permute-start.24 = (bf16[1024,2048]{1,0:T(8,128)(2,1)S(1)}, bf16[1024,2048]{1,0:T(8,128)(2,1)S(1)}, u32[]{:S(2)}, u32[]{:S(2)}) collective-permute-start(bf16[1024,2048]{1,0:T(8,128)(2,1)S(1)} %cat.7.refs_0_), channel_id=1, source_target_pairs={{0,16},{1,17},{2,18},{3,19},{4,20},{5,21},{6,22},{7,23},{8,24},{9,... | collective-permute-start | bytes 12582920 | tf_op jit(solution)/shard_map/ppermute | solution.py:265
  186.0 121.6 %collective-permute-start.32 = (bf16[2048,256]{1,0:T(8,128)(2,1)S(1)}, bf16[2048,256]{1,0:T(8,128)(2,1)S(1)}, u32[]{:S(2)}, u32[]{:S(2)}) collective-permute-start(bf16[2048,256]{1,0:T(8,128)(2,1)S(1)} %step.6.refs_4_.refs_2_), channel_id=1, source_target_pairs={{0,240},{1,241},{2,242},{3,243},{4,244},{5,245},{6,246},{7,247},{8... | collective-permute-start | bytes 3145736 | tf_op jit(solution)/shard_map/ppermute | solution.py:265
  204.2 3.6 %copy-start.7 = (bf16[256,2048]{1,0:T(8,128)(2,1)S(1)}, bf16[256,2048]{1,0:T(8,128)(2,1)}, u32[]{:S(2)}) copy-start(bf16[256,2048]{1,0:T(8,128)(2,1)} %copy-done.5) | copy-start | bytes 3145732
  204.2 102.4 %collective-permute-start.29 = (bf16[2048,256]{1,0:T(8,128)(2,1)S(1)}, bf16[2048,256]{1,0:T(8,128)(2,1)S(1)}, u32[]{:S(2)}, u32[]{:S(2)}) collective-permute-start(bf16[2048,256]{1,0:T(8,128)(2,1)S(1)} %step.9.refs_2_), channel_id=1, source_target_pairs={{0,240},{1,241},{2,242},{3,243},{4,244},{5,245},{6,246},{7,247},{8... | collective-permute-start | bytes 3145736 | tf_op jit(solution)/shard_map/ppermute | solution.py:265
  206.4 110.2 %collective-permute-start.33 = (bf16[2048,256]{1,0:T(8,128)(2,1)S(1)}, bf16[2048,256]{1,0:T(8,128)(2,1)S(1)}, u32[]{:S(2)}, u32[]{:S(2)}) collective-permute-start(bf16[2048,256]{1,0:T(8,128)(2,1)S(1)} %step.11.own), channel_id=1, source_target_pairs={{16,32},{17,33},{18,34},{19,35},{20,36},{21,37},{22,38},{23,39},{2... | collective-permute-start | bytes 3145736 | tf_op jit(solution)/shard_map/ppermute | solution.py:265
  207.7 110.2 %collective-permute-start.31 = (bf16[2048,256]{1,0:T(8,128)(2,1)S(1)}, bf16[2048,256]{1,0:T(8,128)(2,1)S(1)}, u32[]{:S(2)}, u32[]{:S(2)}) collective-permute-start(bf16[2048,256]{1,0:T(8,128)(2,1)S(1)} %step.11.own), channel_id=1, source_target_pairs={{0,16},{1,17},{2,18},{3,19},{4,20},{5,21},{6,22},{7,23},{8,24},{9,... | collective-permute-start | bytes 3145736 | tf_op jit(solution)/shard_map/ppermute | solution.py:265
  216.6 103.9 %collective-permute-start.30 = (bf16[2048,256]{1,0:T(8,128)(2,1)S(1)}, bf16[2048,256]{1,0:T(8,128)(2,1)S(1)}, u32[]{:S(2)}, u32[]{:S(2)}) collective-permute-start(bf16[2048,256]{1,0:T(8,128)(2,1)S(1)} %step.10.own), channel_id=1, source_target_pairs={{16,32},{17,33},{18,34},{19,35},{20,36},{21,37},{22,38},{23,39},{2... | collective-permute-start | bytes 3145736 | tf_op jit(solution)/shard_map/ppermute | solution.py:265
  306.6 13.9 %collective-permute-start.28 = (bf16[2048,256]{1,0:T(8,128)(2,1)S(1)}, bf16[2048,256]{1,0:T(8,128)(2,1)S(1)}, u32[]{:S(2)}, u32[]{:S(2)}) collective-permute-start(bf16[2048,256]{1,0:T(8,128)(2,1)S(1)} %step.10.own), channel_id=1, source_target_pairs={{0,16},{1,17},{2,18},{3,19},{4,20},{5,21},{6,22},{7,23},{8,24},{9,... | collective-permute-start | bytes 3145736 | tf_op jit(solution)/shard_map/ppermute | solution.py:265
  307.6 32.4 %collective-permute-start.26 = (bf16[2048,256]{1,0:T(8,128)(2,1)S(1)}, bf16[2048,256]{1,0:T(8,128)(2,1)S(1)}, u32[]{:S(2)}, u32[]{:S(2)}) collective-permute-start(bf16[2048,256]{1,0:T(8,128)(2,1)S(1)} %step.7.refs_2_), channel_id=1, source_target_pairs={{0,240},{1,241},{2,242},{3,243},{4,244},{5,245},{6,246},{7,247},{8... | collective-permute-start | bytes 3145736 | tf_op jit(solution)/shard_map/ppermute | solution.py:265
  316.6 24.4 %collective-permute-start.27 = (bf16[2048,256]{1,0:T(8,128)(2,1)S(1)}, bf16[2048,256]{1,0:T(8,128)(2,1)S(1)}, u32[]{:S(2)}, u32[]{:S(2)}) collective-permute-start(bf16[2048,256]{1,0:T(8,128)(2,1)S(1)} %step.8.own), channel_id=1, source_target_pairs={{16,32},{17,33},{18,34},{19,35},{20,36},{21,37},{22,38},{23,39},{2... | collective-permute-start | bytes 3145736 | tf_op jit(solution)/shard_map/ppermute | solution.py:265
  318.0 23.1 %collective-permute-start.25 = (bf16[2048,256]{1,0:T(8,128)(2,1)S(1)}, bf16[2048,256]{1,0:T(8,128)(2,1)S(1)}, u32[]{:S(2)}, u32[]{:S(2)}) collective-permute-start(bf16[2048,256]{1,0:T(8,128)(2,1)S(1)} %step.8.own), channel_id=1, source_target_pairs={{0,16},{1,17},{2,18},{3,19},{4,20},{5,21},{6,22},{7,23},{8,24},{9,... | collective-permute-start | bytes 3145736 | tf_op jit(solution)/shard_map/ppermute | solution.py:265

commit v3 on v2

--- a/solution.py
+++ b/solution.py
@@ -185,9 +185,11 @@
 
         lax.fori_loop(0, w.shape[0] // part, band, 0)
 
-    if other is not None:
-        @pl.when(meta[0] != which)
-        def _():
+    @pl.when(meta[0] != which)
+    def _():
+        if other is None:
+            out[...] = jnp.zeros(out.shape, out.dtype)
+        else:
             pltpu.sync_copy(other, out)
 
 
@@ -292,14 +294,17 @@
     w = pack_weights(w_gate[0], w_up[0])
     r1 = along_z(half_a, 1)
     own_a = fan(half_a)
+    b1 = along_z(half_b, 1)
     r2 = along_z(r1, 1)
     one_a = fan(r1)
+    b2 = along_z(b1, 1)
     r3 = along_z(r2, 1)
-    two_a = fan(r2)
     hg = split_units(hidden_grad[0], NZ * NX)
     hg = lax.all_to_all(hg, "dp", split_axis=0, concat_axis=0, tiled=True)
+    b3 = along_z(b2, 1)
+    two_a = fan(r2)
     three_a = fan(r3)
-    column_b = [along_z(half_b, k) for k in range(1, NZ)]
+    column_b = [b1, b2, b3]
     early = cat(own_a + one_a + two_a)
     late = cat(three_a)
     pieces = [early, late, swap(early), swap(late)]
@@ -307,14 +312,14 @@
     step_a, cross_a = [], []
     for c in range(CHUNKS):
         step_a.append(step_chunk(0, c, meta_a, hg, w, pieces))
-        cross_a.append(send(step_a[c], lambda g, u, t: (g - 1, u, t) if g % 2 == 0 else None))
+        cross_a.append(send(step_a[c], lambda g, u, t: (g - 1, u, t)))
 
     blocks = cat(fan(cat([half_b] + column_b, step_a[0])))
     blocks = [blocks, swap(blocks)]
     mine, cross_b, near = [], [], []
     for c in range(CHUNKS):
         mine.append(step_chunk(1, c, meta_b, hg, w, blocks, step_a[c]))
-        cross_b.append(send(mine[c], lambda g, u, t: (g + 1, u, t) if g % 2 == 1 else None))
+        cross_b.append(send(mine[c], lambda g, u, t: (g + 1, u, t)))
         near.append(swap(mine[c]))
 
     done = None

time: 344 us -> 336 us (0.977)
  the two profiles are of different devices: /device:TPU:38 before, /device:TPU:2 now
where the time goes in v3:
time: 336 us; the launch traced here: 335 us
  waiting for transfers between devices  214 us (64%)
  starting transfers between devices  72.3 us (22%)
  Pallas kernels  38 us (11%)
  local copies, waits for them, and re-layouts  9.55 us (3%)
    ppermute x34, waiting for transfers between devices, send(): return lax.ppermute(v, axes, device_pairs(groups, move))  214 us
    ppermute x34, starting transfers between devices, send(): return lax.ppermute(v, axes, device_pairs(groups, move))  64.6 us
    pallas_call x6, Pallas kernels, step_chunk(): pl.pallas_call(functools.partial(step_body, which, len(xs), c), grid=(1,)...  25.9 us
    unnamed x34, local copies, waits for them, and re-layouts  9.55 us
    all_to_all x1, starting transfers between devices, local(): hg = lax.all_to_all(hg, 'dp', split_axis=0, concat_axis=0, tiled=True)  7.75 us
    pallas_call x3, Pallas kernels, mix_chunk(): pl.pallas_call(mix_body, grid=(width // band,), out_shape=(jax.ShapeDtype...  7.25 us
  transfers between devices with their start and end apart: 35, of which 20 were waited for; matrix products, arithmetic and copies ran while one was open for 0% of the time, Pallas kernels for 10%

profile of v3, /device:TPU:2, one launch (start us, length us, event | category | flops | bytes accessed | tf_op | source)
XLA Modules:
  0.0 335.4 jit_solution(2182120910320713183)
XLA Ops:
  0.8 0.7 fusion
  1.5 1.3 collective-permute-done.got
  2.8 1.0 copy-done.8
  3.9 0.6 pick.1
  4.5 2.0 collective-permute-start.7
  6.5 2.1 collective-permute-start.6
  8.6 1.4 collective-permute-start.5
  10.1 5.8 %collective-permute-done.7.refs_4_ = bf16[64,2048]{1,0:T(8,128)(2,1)S(1)} collective-permute-done((bf16[64,2048]{1,0:T(8,128)(2,1)S(1)}, bf16[64,2048]{1,0:T(8,128)(2,1)S(1)}, u32[]{:S(2)}, u32[]{:S(2)}) %collective-permute-start.7) | collective-permute-done | bytes 262176 | tf_op jit(solution)/shard_map/ppermute | solution.py:267
  15.8 1.5 collective-permute-start.4
  17.3 1.7 collective-permute-start.10
  19.1 1.5 collective-permute-start.9
  20.6 2.3 collective-permute-done.5.refs_2_
  22.8 0.5 collective-permute-start.8
  23.3 2.0 collective-permute-done.11.refs_8_
  25.4 2.1 collective-permute-start.14
  27.5 1.4 collective-permute-start.13
  29.0 3.2 collective-permute-start.12
  32.1 2.0 collective-permute-done.9.refs_6_
  34.1 4.4 %collective-permute-done.8.refs_5_ = bf16[64,2048]{1,0:T(8,128)(2,1)S(1)} collective-permute-done((bf16[64,2048]{1,0:T(8,128)(2,1)S(1)}, bf16[64,2048]{1,0:T(8,128)(2,1)S(1)}, u32[]{:S(2)}, u32[]{:S(2)}) %collective-permute-start.8) | collective-permute-done | bytes 262176 | tf_op jit(solution)/shard_map/ppermute | solution.py:267
  38.5 1.2 collective-permute-done.14.refs_11_
  39.7 4.4 %collective-permute-done.13.refs_10_ = bf16[64,2048]{1,0:T(8,128)(2,1)S(1)} collective-permute-done((bf16[64,2048]{1,0:T(8,128)(2,1)S(1)}, bf16[64,2048]{1,0:T(8,128)(2,1)S(1)}, u32[]{:S(2)}, u32[]{:S(2)}) %collective-permute-start.13) | collective-permute-done | bytes 262176 | tf_op jit(solution)/shard_map/ppermute | solution.py:267
  44.2 2.0 collective-permute-done.12.refs_9_
  46.6 1.3 split.1
  47.9 7.7 %all-to-all-start = ((bf16[16,128,384]{2,1,0:T(8,128)(2,1)}), bf16[16,128,384]{2,1,0:T(8,128)(2,1)}, u32[]{:S(2)}, u32[]{:S(2)}) async-start(bf16[16,128,384]{2,1,0:T(8,128)(2,1)} %split.1), calls=%async_computation | async-start | bytes 3145728 | tf_op jit(solution)/shard_map/all_to_all | solution.py:303
  55.7 1.5 collective-permute-start.15
  57.2 33.8 %collective-permute-done.15.refs_0_ = bf16[64,2048]{1,0:T(8,128)(2,1)S(1)} collective-permute-done((bf16[64,2048]{1,0:T(8,128)(2,1)}, bf16[64,2048]{1,0:T(8,128)(2,1)S(1)}, u32[]{:S(2)}, u32[]{:S(2)}) %collective-permute-start.15) | collective-permute-done | bytes 262176 | tf_op jit(solution)/shard_map/ppermute | solution.py:267
  91.0 2.2 collective-permute-start.18
  93.2 1.5 collective-permute-start.17
  94.7 0.6 collective-permute-start.16
  95.2 6.8 %collective-permute-done.18.refs_3_ = bf16[64,2048]{1,0:T(8,128)(2,1)S(1)} collective-permute-done((bf16[64,2048]{1,0:T(8,128)(2,1)S(1)}, bf16[64,2048]{1,0:T(8,128)(2,1)S(1)}, u32[]{:S(2)}, u32[]{:S(2)}) %collective-permute-start.18) | collective-permute-done | bytes 262176 | tf_op jit(solution)/shard_map/ppermute | solution.py:267
  102.0 4.0 %collective-permute-done.17.refs_2_ = bf16[64,2048]{1,0:T(8,128)(2,1)S(1)} collective-permute-done((bf16[64,2048]{1,0:T(8,128)(2,1)S(1)}, bf16[64,2048]{1,0:T(8,128)(2,1)S(1)}, u32[]{:S(2)}, u32[]{:S(2)}) %collective-permute-start.17) | collective-permute-done | bytes 262176 | tf_op jit(solution)/shard_map/ppermute | solution.py:267
  106.3 5.9 %collective-permute-start.1 = (bf16[64,2048]{1,0:T(8,128)(2,1)S(1)}, bf16[64,2048]{1,0:T(8,128)(2,1)S(1)}, u32[]{:S(2)}, u32[]{:S(2)}) collective-permute-start(bf16[64,2048]{1,0:T(8,128)(2,1)S(1)} %get-tuple-element.10.refs_0_), channel_id=1, source_target_pairs={{0,4},{1,5},{2,6},{3,7},{4,8},{5,9},{6,10},{7,11},{8,12},{9,13},{1... | collective-permute-start | bytes 786440 | tf_op jit(solution)/shard_map/ppermute | solution.py:267
  112.2 6.1 %collective-permute-done.1.refs_1_ = bf16[64,2048]{1,0:T(8,128)(2,1)S(1)} collective-permute-done((bf16[64,2048]{1,0:T(8,128)(2,1)S(1)}, bf16[64,2048]{1,0:T(8,128)(2,1)S(1)}, u32[]{:S(2)}, u32[]{:S(2)}) %collective-permute-start.1) | collective-permute-done | bytes 262176 | tf_op jit(solution)/shard_map/ppermute | solution.py:267
  118.3 2.5 collective-permute-start.2
  120.8 1.4 copy-done.4
  122.2 1.2 pack.1.packed
  123.4 1.7 copy-done
  125.1 3.7 %collective-permute-done.2.refs_2_ = bf16[64,2048]{1,0:T(8,128)(2,1)} collective-permute-done((bf16[64,2048]{1,0:T(8,128)(2,1)S(1)}, bf16[64,2048]{1,0:T(8,128)(2,1)}, u32[]{:S(2)}, u32[]{:S(2)}) %collective-permute-start.2) | collective-permute-done | bytes 262176 | tf_op jit(solution)/shard_map/ppermute | solution.py:267
  128.8 1.0 copy-done.12
  129.8 1.9 copy-done.1
  131.7 1.2 copy-done.6
  132.9 1.2 copy-done.13
  134.2 7.9 %step.6.refs_4_.refs_2_ = bf16[2048,256]{1,0:T(8,128)(2,1)S(1)} custom-call(s32[17]{0:T(128)S(1)} %pad_add_fusion.meta, bf16[16,128,384]{2,1,0:T(8,128)(2,1)} %all-to-all-done.units, bf16[3,2048,256]{2,1,0:T(8,128)(2,1)S(1)} %copy-done.1, bf16[768,2048]{1,0:T(8,128)(2,1)S(1)} %cat.4.refs_0_, bf16[256,2048]{1,0:T(8,128)(2,1)S(1)} %copy-done.6, ...), custom_call_target="tpu_custom_call" | custom-call | flops 4294967296 | bytes 8388608 | tf_op jit(solution)/shard_map/step/pallas_call | solution.py:200
  142.1 1.1 cat.6.refs_0_
  143.2 2.1 collective-permute-start.23
  145.3 1.5 collective-permute-start.22
  146.8 0.6 collective-permute-start.21
  147.3 23.5 %collective-permute-done.23.refs_3_ = bf16[256,2048]{1,0:T(8,128)(2,1)S(1)} collective-permute-done((bf16[256,2048]{1,0:T(8,128)(2,1)S(1)}, bf16[256,2048]{1,0:T(8,128)(2,1)S(1)}, u32[]{:S(2)}, u32[]{:S(2)}) %collective-permute-start.23) | collective-permute-done | bytes 1048608 | tf_op jit(solution)/shard_map/ppermute | solution.py:267
  170.8 16.2 %collective-permute-done.22.refs_2_ = bf16[256,2048]{1,0:T(8,128)(2,1)S(1)} collective-permute-done((bf16[256,2048]{1,0:T(8,128)(2,1)S(1)}, bf16[256,2048]{1,0:T(8,128)(2,1)S(1)}, u32[]{:S(2)}, u32[]{:S(2)}) %collective-permute-start.22) | collective-permute-done | bytes 1048608 | tf_op jit(solution)/shard_map/ppermute | solution.py:267
  187.6 8.4 %collective-permute-start.32 = (bf16[2048,256]{1,0:T(8,128)(2,1)S(1)}, bf16[2048,256]{1,0:T(8,128)(2,1)S(1)}, u32[]{:S(2)}, u32[]{:S(2)}) collective-permute-start(bf16[2048,256]{1,0:T(8,128)(2,1)S(1)} %step.6.refs_4_.refs_2_), channel_id=1, source_target_pairs={{0,240},{1,241},{2,242},{3,243},{4,244},{5,245},{6,246},{7,247},{8... | collective-permute-start | bytes 3145736 | tf_op jit(solution)/shard_map/ppermute | solution.py:267
  196.0 7.9 %step.9.refs_2_ = bf16[2048,256]{1,0:T(8,128)(2,1)S(1)} custom-call(s32[17]{0:T(128)S(1)} %pad_add_fusion.meta, bf16[16,128,384]{2,1,0:T(8,128)(2,1)} %all-to-all-done.units, bf16[3,2048,256]{2,1,0:T(8,128)(2,1)S(1)} %copy-done.1, bf16[768,2048]{1,0:T(8,128)(2,1)S(1)} %cat.4.refs_0_, bf16[256,2048]{1,0:T(8,128)(2,1)S(1)} %copy-done.6, ...), custom_call_target="tpu_custom_call" | custom-call | flops 4294967296 | bytes 8388608 | tf_op jit(solution)/shard_map/step/pallas_call | solution.py:200
  204.0 0.9 step.11.own
  204.9 7.7 %collective-permute-start.33 = (bf16[2048,256]{1,0:T(8,128)(2,1)S(1)}, bf16[2048,256]{1,0:T(8,128)(2,1)S(1)}, u32[]{:S(2)}, u32[]{:S(2)}) collective-permute-start(bf16[2048,256]{1,0:T(8,128)(2,1)S(1)} %step.11.own), channel_id=1, source_target_pairs={{0,16},{1,17},{2,18},{3,19},{4,20},{5,21},{6,22},{7,23},{8,24},{9,... | collective-permute-start | bytes 3145736 | tf_op jit(solution)/shard_map/ppermute | solution.py:267
  212.7 7.9 %step.7.refs_2_ = bf16[2048,256]{1,0:T(8,128)(2,1)S(1)} custom-call(s32[17]{0:T(128)S(1)} %pad_add_fusion.meta, bf16[16,128,384]{2,1,0:T(8,128)(2,1)} %all-to-all-done.units, bf16[3,2048,256]{2,1,0:T(8,128)(2,1)S(1)} %copy-done.1, bf16[768,2048]{1,0:T(8,128)(2,1)S(1)} %cat.4.refs_0_, bf16[256,2048]{1,0:T(8,128)(2,1)S(1)} %copy-done.7, ...), custom_call_target="tpu_custom_call" | custom-call | flops 4294967296 | bytes 8388608 | tf_op jit(solution)/shard_map/step/pallas_call | solution.py:200
  220.6 0.7 step.10.own
  221.8 0.7 step.8.own
  222.4 72.6 %collective-permute-done.29.far_a = bf16[2048,256]{1,0:T(8,128)(2,1)S(1)} collective-permute-done((bf16[2048,256]{1,0:T(8,128)(2,1)S(1)}, bf16[2048,256]{1,0:T(8,128)(2,1)S(1)}, u32[]{:S(2)}, u32[]{:S(2)}) %collective-permute-start.29) | collective-permute-done | bytes 1048608 | tf_op jit(solution)/shard_map/ppermute | solution.py:267
  295.1 11.5 %collective-permute-start.26 = (bf16[2048,256]{1,0:T(8,128)(2,1)S(1)}, bf16[2048,256]{1,0:T(8,128)(2,1)S(1)}, u32[]{:S(2)}, u32[]{:S(2)}) collective-permute-start(bf16[2048,256]{1,0:T(8,128)(2,1)S(1)} %step.7.refs_2_), channel_id=1, source_target_pairs={{0,240},{1,241},{2,242},{3,243},{4,244},{5,245},{6,246},{7,247},{8... | collective-permute-start | bytes 3145736 | tf_op jit(solution)/shard_map/ppermute | solution.py:267
  306.7 2.4 mix.3
  309.1 3.0 collective-permute-done.30.far_b
  312.1 2.4 mix.4
  314.5 15.2 %collective-permute-done.26.far_a = bf16[2048,256]{1,0:T(8,128)(2,1)S(1)} collective-permute-done((bf16[2048,256]{1,0:T(8,128)(2,1)S(1)}, bf16[2048,256]{1,0:T(8,128)(2,1)S(1)}, u32[]{:S(2)}, u32[]{:S(2)}) %collective-permute-start.26) | collective-permute-done | bytes 1048608 | tf_op jit(solution)/shard_map/ppermute | solution.py:267
  329.7 3.3 collective-permute-done.27.far_b
  333.0 2.4 mix.5
  (60 shorter events, 2.2 us)
Async XLA Ops:
  0.6 2.2 collective-permute-start
  2.8 1.0 copy-start.8
  4.5 42.1 %copy-start.2 = (bf16[1,128,6144]{2,1,0:T(8,128)(2,1)S(1)}, bf16[1,128,6144]{2,1,0:T(8,128)(2,1)}, u32[]{:S(2)}) copy-start(bf16[1,128,6144]{2,1,0:T(8,128)(2,1)} %param.9) | copy-start | bytes 4718596
  4.5 11.3 %collective-permute-start.7 = (bf16[64,2048]{1,0:T(8,128)(2,1)S(1)}, bf16[64,2048]{1,0:T(8,128)(2,1)S(1)}, u32[]{:S(2)}, u32[]{:S(2)}) collective-permute-start(bf16[64,2048]{1,0:T(8,128)(2,1)S(1)} %get-tuple-element.11.refs_0_), channel_id=1, source_target_pairs={{0,4},{1,5},{2,6},{3,7},{4,8},{5,9},{6,10},{7,11},{8,12},{9,13},{1... | collective-permute-start | bytes 786440 | tf_op jit(solution)/shard_map/ppermute | solution.py:267
  6.5 12.5 %collective-permute-start.6 = (bf16[64,2048]{1,0:T(8,128)(2,1)S(1)}, bf16[64,2048]{1,0:T(8,128)(2,1)S(1)}, u32[]{:S(2)}, u32[]{:S(2)}) collective-permute-start(bf16[64,2048]{1,0:T(8,128)(2,1)S(1)} %get-tuple-element.11.refs_0_), channel_id=1, source_target_pairs={{0,2},{1,3},{2,0},{3,1},{4,6},{5,7},{6,4},{7,5},{8,10},{9,11},{10,... | collective-permute-start | bytes 786440 | tf_op jit(solution)/shard_map/ppermute | solution.py:267
  8.6 14.2 %collective-permute-start.5 = (bf16[64,2048]{1,0:T(8,128)(2,1)S(1)}, bf16[64,2048]{1,0:T(8,128)(2,1)S(1)}, u32[]{:S(2)}, u32[]{:S(2)}) collective-permute-start(bf16[64,2048]{1,0:T(8,128)(2,1)S(1)} %get-tuple-element.11.refs_0_), channel_id=1, source_target_pairs={{0,3},{1,0},{2,1},{3,2},{4,7},{5,4},{6,5},{7,6},{8,11},{9,8},{10,9... | collective-permute-start | bytes 786440 | tf_op jit(solution)/shard_map/ppermute | solution.py:267
  15.8 9.6 %collective-permute-start.11 = (bf16[64,2048]{1,0:T(8,128)(2,1)S(1)}, bf16[64,2048]{1,0:T(8,128)(2,1)S(1)}, u32[]{:S(2)}, u32[]{:S(2)}) collective-permute-start(bf16[64,2048]{1,0:T(8,128)(2,1)S(1)} %collective-permute-done.7.refs_4_), channel_id=1, source_target_pairs={{0,4},{1,5},{2,6},{3,7},{4,8},{5,9},{6,10},{7,11},{8,12},{9,13},{1... | collective-permute-start | bytes 786440 | tf_op jit(solution)/shard_map/ppermute | solution.py:267
  15.8 11.7 %collective-permute-start.4 = (bf16[64,2048]{1,0:T(8,128)(2,1)S(1)}, bf16[64,2048]{1,0:T(8,128)(2,1)S(1)}, u32[]{:S(2)}, u32[]{:S(2)}) collective-permute-start(bf16[64,2048]{1,0:T(8,128)(2,1)S(1)} %get-tuple-element.11.refs_0_), channel_id=1, source_target_pairs={{0,1},{1,2},{2,3},{3,0},{4,5},{5,6},{6,7},{7,4},{8,9},{9,10},{10,1... | collective-permute-start | bytes 786440 | tf_op jit(solution)/shard_map/ppermute | solution.py:267
  17.3 11.6 %collective-permute-start.10 = (bf16[64,2048]{1,0:T(8,128)(2,1)S(1)}, bf16[64,2048]{1,0:T(8,128)(2,1)S(1)}, u32[]{:S(2)}, u32[]{:S(2)}) collective-permute-start(bf16[64,2048]{1,0:T(8,128)(2,1)S(1)} %collective-permute-done.7.refs_4_), channel_id=1, source_target_pairs={{0,2},{1,3},{2,0},{3,1},{4,6},{5,7},{6,4},{7,5},{8,10},{9,11},{10,... | collective-permute-start | bytes 786440 | tf_op jit(solution)/shard_map/ppermute | solution.py:267
  19.1 15.0 %collective-permute-start.9 = (bf16[64,2048]{1,0:T(8,128)(2,1)S(1)}, bf16[64,2048]{1,0:T(8,128)(2,1)S(1)}, u32[]{:S(2)}, u32[]{:S(2)}) collective-permute-start(bf16[64,2048]{1,0:T(8,128)(2,1)S(1)} %collective-permute-done.7.refs_4_), channel_id=1, source_target_pairs={{0,3},{1,0},{2,1},{3,2},{4,7},{5,4},{6,5},{7,6},{8,11},{9,8},{10,9... | collective-permute-start | bytes 786440 | tf_op jit(solution)/shard_map/ppermute | solution.py:267
  22.8 15.7 %collective-permute-start.8 = (bf16[64,2048]{1,0:T(8,128)(2,1)S(1)}, bf16[64,2048]{1,0:T(8,128)(2,1)S(1)}, u32[]{:S(2)}, u32[]{:S(2)}) collective-permute-start(bf16[64,2048]{1,0:T(8,128)(2,1)S(1)} %collective-permute-done.7.refs_4_), channel_id=1, source_target_pairs={{0,1},{1,2},{2,3},{3,0},{4,5},{5,6},{6,7},{7,4},{8,9},{9,10},{10,1... | collective-permute-start | bytes 786440 | tf_op jit(solution)/shard_map/ppermute | solution.py:267
  25.4 21.1 %copy-start.9 = (bf16[64,2048]{1,0:T(8,128)(2,1)}, bf16[64,2048]{1,0:T(8,128)(2,1)S(1)}, u32[]{:S(2)}) copy-start(bf16[64,2048]{1,0:T(8,128)(2,1)S(1)} %collective-permute-done.11.refs_8_) | copy-start | bytes 786436
  25.4 14.3 %collective-permute-start.14 = (bf16[64,2048]{1,0:T(8,128)(2,1)S(1)}, bf16[64,2048]{1,0:T(8,128)(2,1)S(1)}, u32[]{:S(2)}, u32[]{:S(2)}) collective-permute-start(bf16[64,2048]{1,0:T(8,128)(2,1)S(1)} %collective-permute-done.11.refs_8_), channel_id=1, source_target_pairs={{0,2},{1,3},{2,0},{3,1},{4,6},{5,7},{6,4},{7,5},{8,10},{9,11},{10,... | collective-permute-start | bytes 786440 | tf_op jit(solution)/shard_map/ppermute | solution.py:267
  27.5 16.6 %collective-permute-start.13 = (bf16[64,2048]{1,0:T(8,128)(2,1)S(1)}, bf16[64,2048]{1,0:T(8,128)(2,1)S(1)}, u32[]{:S(2)}, u32[]{:S(2)}) collective-permute-start(bf16[64,2048]{1,0:T(8,128)(2,1)S(1)} %collective-permute-done.11.refs_8_), channel_id=1, source_target_pairs={{0,3},{1,0},{2,1},{3,2},{4,7},{5,4},{6,5},{7,6},{8,11},{9,8},{10,9... | collective-permute-start | bytes 786440 | tf_op jit(solution)/shard_map/ppermute | solution.py:267
  29.0 17.2 %collective-permute-start.12 = (bf16[64,2048]{1,0:T(8,128)(2,1)S(1)}, bf16[64,2048]{1,0:T(8,128)(2,1)S(1)}, u32[]{:S(2)}, u32[]{:S(2)}) collective-permute-start(bf16[64,2048]{1,0:T(8,128)(2,1)S(1)} %collective-permute-done.11.refs_8_), channel_id=1, source_target_pairs={{0,1},{1,2},{2,3},{3,0},{4,5},{5,6},{6,7},{7,4},{8,9},{9,10},{10,1... | collective-permute-start | bytes 786440 | tf_op jit(solution)/shard_map/ppermute | solution.py:267
  46.5 83.3 %collective-permute-start.19 = (bf16[768,2048]{1,0:T(8,128)(2,1)S(1)}, bf16[768,2048]{1,0:T(8,128)(2,1)}, u32[]{:S(2)}, u32[]{:S(2)}) collective-permute-start(bf16[768,2048]{1,0:T(8,128)(2,1)S(1)} %cat.4.refs_0_), channel_id=1, source_target_pairs={{0,16},{1,17},{2,18},{3,19},{4,20},{5,21},{6,22},{7,23},{8,24},{9,... | collective-permute-start | bytes 9437192 | tf_op jit(solution)/shard_map/ppermute | solution.py:267
  47.9 81.9 %all-to-all-start = ((bf16[16,128,384]{2,1,0:T(8,128)(2,1)}), bf16[16,128,384]{2,1,0:T(8,128)(2,1)}, u32[]{:S(2)}, u32[]{:S(2)}) async-start(bf16[16,128,384]{2,1,0:T(8,128)(2,1)} %split.1), calls=%async_computation | async-start | bytes 3145728 | tf_op jit(solution)/shard_map/all_to_all | solution.py:303
  55.7 65.2 %copy-start.3 = (bf16[1,2048,384]{2,1,0:T(8,128)(2,1)S(1)}, bf16[1,2048,384]{2,1,0:T(8,128)(2,1)}, u32[]{:S(2)}) copy-start(bf16[1,2048,384]{2,1,0:T(8,128)(2,1)} %param.10) | copy-start | bytes 4718596
  55.7 35.4 %collective-permute-start.15 = (bf16[64,2048]{1,0:T(8,128)(2,1)}, bf16[64,2048]{1,0:T(8,128)(2,1)S(1)}, u32[]{:S(2)}, u32[]{:S(2)}) collective-permute-start(bf16[64,2048]{1,0:T(8,128)(2,1)} %copy-done.9), channel_id=1, source_target_pairs={{0,4},{1,5},{2,6},{3,7},{4,8},{5,9},{6,10},{7,11},{8,12},{9,13},{1... | collective-permute-start | bytes 786440 | tf_op jit(solution)/shard_map/ppermute | solution.py:267
  91.0 11.0 %collective-permute-start.18 = (bf16[64,2048]{1,0:T(8,128)(2,1)S(1)}, bf16[64,2048]{1,0:T(8,128)(2,1)S(1)}, u32[]{:S(2)}, u32[]{:S(2)}) collective-permute-start(bf16[64,2048]{1,0:T(8,128)(2,1)S(1)} %collective-permute-done.15.refs_0_), channel_id=1, source_target_pairs={{0,2},{1,3},{2,0},{3,1},{4,6},{5,7},{6,4},{7,5},{8,10},{9,11},{10,... | collective-permute-start | bytes 786440 | tf_op jit(solution)/shard_map/ppermute | solution.py:267
  93.2 12.8 %collective-permute-start.17 = (bf16[64,2048]{1,0:T(8,128)(2,1)S(1)}, bf16[64,2048]{1,0:T(8,128)(2,1)S(1)}, u32[]{:S(2)}, u32[]{:S(2)}) collective-permute-start(bf16[64,2048]{1,0:T(8,128)(2,1)S(1)} %collective-permute-done.15.refs_0_), channel_id=1, source_target_pairs={{0,3},{1,0},{2,1},{3,2},{4,7},{5,4},{6,5},{7,6},{8,11},{9,8},{10,9... | collective-permute-start | bytes 786440 | tf_op jit(solution)/shard_map/ppermute | solution.py:267
  94.7 11.4 %collective-permute-start.16 = (bf16[64,2048]{1,0:T(8,128)(2,1)S(1)}, bf16[64,2048]{1,0:T(8,128)(2,1)S(1)}, u32[]{:S(2)}, u32[]{:S(2)}) collective-permute-start(bf16[64,2048]{1,0:T(8,128)(2,1)S(1)} %collective-permute-done.15.refs_0_), channel_id=1, source_target_pairs={{0,1},{1,2},{2,3},{3,0},{4,5},{5,6},{6,7},{7,4},{8,9},{9,10},{10,1... | collective-permute-start | bytes 786440 | tf_op jit(solution)/shard_map/ppermute | solution.py:267
  106.1 17.2 %copy-start.5 = (bf16[256,2048]{1,0:T(8,128)(2,1)}, bf16[256,2048]{1,0:T(8,128)(2,1)S(1)}, u32[]{:S(2)}) copy-start(bf16[256,2048]{1,0:T(8,128)(2,1)S(1)} %cat.5.refs_1_) | copy-start | bytes 3145732
  106.2 22.6 %collective-permute-start.20 = (bf16[256,2048]{1,0:T(8,128)(2,1)S(1)}, bf16[256,2048]{1,0:T(8,128)(2,1)S(1)}, u32[]{:S(2)}, u32[]{:S(2)}) collective-permute-start(bf16[256,2048]{1,0:T(8,128)(2,1)S(1)} %cat.5.refs_1_), channel_id=1, source_target_pairs={{0,16},{1,17},{2,18},{3,19},{4,20},{5,21},{6,22},{7,23},{8,24},{9,... | collective-permute-start | bytes 3145736 | tf_op jit(solution)/shard_map/ppermute | solution.py:267
  106.3 12.1 %collective-permute-start.1 = (bf16[64,2048]{1,0:T(8,128)(2,1)S(1)}, bf16[64,2048]{1,0:T(8,128)(2,1)S(1)}, u32[]{:S(2)}, u32[]{:S(2)}) collective-permute-start(bf16[64,2048]{1,0:T(8,128)(2,1)S(1)} %get-tuple-element.10.refs_0_), channel_id=1, source_target_pairs={{0,4},{1,5},{2,6},{3,7},{4,8},{5,9},{6,10},{7,11},{8,12},{9,13},{1... | collective-permute-start | bytes 786440 | tf_op jit(solution)/shard_map/ppermute | solution.py:267
  118.3 5.1 %copy-start.10 = (bf16[64,2048]{1,0:T(8,128)(2,1)}, bf16[64,2048]{1,0:T(8,128)(2,1)S(1)}, u32[]{:S(2)}) copy-start(bf16[64,2048]{1,0:T(8,128)(2,1)S(1)} %collective-permute-done.1.refs_1_) | copy-start | bytes 786436
  118.3 10.4 %collective-permute-start.2 = (bf16[64,2048]{1,0:T(8,128)(2,1)S(1)}, bf16[64,2048]{1,0:T(8,128)(2,1)}, u32[]{:S(2)}, u32[]{:S(2)}) collective-permute-start(bf16[64,2048]{1,0:T(8,128)(2,1)S(1)} %collective-permute-done.1.refs_1_), channel_id=1, source_target_pairs={{0,4},{1,5},{2,6},{3,7},{4,8},{5,9},{6,10},{7,11},{8,12},{9,13},{1... | collective-permute-start | bytes 786440 | tf_op jit(solution)/shard_map/ppermute | solution.py:267
  120.8 1.4 copy-start.4
  123.4 1.7 copy-start
  128.8 13.3 %collective-permute-start.3 = (bf16[64,2048]{1,0:T(8,128)(2,1)}, bf16[64,2048]{1,0:T(8,128)(2,1)}, u32[]{:S(2)}, u32[]{:S(2)}) collective-permute-start(bf16[64,2048]{1,0:T(8,128)(2,1)} %collective-permute-done.2.refs_2_), channel_id=1, source_target_pairs={{0,4},{1,5},{2,6},{3,7},{4,8},{5,9},{6,10},{7,11},{8,12},{9,13},{1... | collective-permute-start | bytes 786440 | tf_op jit(solution)/shard_map/ppermute | solution.py:267
  128.8 1.0 copy-start.12
  129.8 1.9 copy-start.1
  131.7 1.2 copy-start.6
  132.9 1.2 copy-start.13
  134.2 7.9 %copy-start.11 = (bf16[64,2048]{1,0:T(8,128)(2,1)S(1)}, bf16[64,2048]{1,0:T(8,128)(2,1)}, u32[]{:S(2)}) copy-start(bf16[64,2048]{1,0:T(8,128)(2,1)} %copy-done.10) | copy-start | bytes 786436
  143.2 44.3 %copy-start.15 = (s32[16]{0:T(128)S(1)}, s32[16]{0:T(128)}, u32[]{:S(2)}) copy-start(s32[16]{0:T(128)} %constant.84) | copy-start | bytes 196
  143.2 44.3 %copy-start.16 = (s32[16]{0:T(128)S(1)}, s32[16]{0:T(128)}, u32[]{:S(2)}) copy-start(s32[16]{0:T(128)} %constant.83) | copy-start | bytes 196
  143.2 52.8 %copy-start.14 = (bf16[256,2048]{1,0:T(8,128)(2,1)S(1)}, bf16[256,2048]{1,0:T(8,128)(2,1)}, u32[]{:S(2)}) copy-start(bf16[256,2048]{1,0:T(8,128)(2,1)} %copy-done.12) | copy-start | bytes 3145732
  143.2 27.6 %collective-permute-start.23 = (bf16[256,2048]{1,0:T(8,128)(2,1)S(1)}, bf16[256,2048]{1,0:T(8,128)(2,1)S(1)}, u32[]{:S(2)}, u32[]{:S(2)}) collective-permute-start(bf16[256,2048]{1,0:T(8,128)(2,1)S(1)} %cat.6.refs_0_), channel_id=1, source_target_pairs={{0,2},{1,3},{2,0},{3,1},{4,6},{5,7},{6,4},{7,5},{8,10},{9,11},{10,... | collective-permute-start | bytes 3145736 | tf_op jit(solution)/shard_map/ppermute | solution.py:267
  145.3 41.7 %collective-permute-start.22 = (bf16[256,2048]{1,0:T(8,128)(2,1)S(1)}, bf16[256,2048]{1,0:T(8,128)(2,1)S(1)}, u32[]{:S(2)}, u32[]{:S(2)}) collective-permute-start(bf16[256,2048]{1,0:T(8,128)(2,1)S(1)} %cat.6.refs_0_), channel_id=1, source_target_pairs={{0,3},{1,0},{2,1},{3,2},{4,7},{5,4},{6,5},{7,6},{8,11},{9,8},{10,9... | collective-permute-start | bytes 3145736 | tf_op jit(solution)/shard_map/ppermute | solution.py:267
  146.8 40.3 %collective-permute-start.21 = (bf16[256,2048]{1,0:T(8,128)(2,1)S(1)}, bf16[256,2048]{1,0:T(8,128)(2,1)S(1)}, u32[]{:S(2)}, u32[]{:S(2)}) collective-permute-start(bf16[256,2048]{1,0:T(8,128)(2,1)S(1)} %cat.6.refs_0_), channel_id=1, source_target_pairs={{0,1},{1,2},{2,3},{3,0},{4,5},{5,6},{6,7},{7,4},{8,9},{9,10},{10,1... | collective-permute-start | bytes 3145736 | tf_op jit(solution)/shard_map/ppermute | solution.py:267
  187.4 16.6 %collective-permute-start.24 = (bf16[1024,2048]{1,0:T(8,128)(2,1)S(1)}, bf16[1024,2048]{1,0:T(8,128)(2,1)S(1)}, u32[]{:S(2)}, u32[]{:S(2)}) collective-permute-start(bf16[1024,2048]{1,0:T(8,128)(2,1)S(1)} %cat.7.refs_0_), channel_id=1, source_target_pairs={{0,16},{1,17},{2,18},{3,19},{4,20},{5,21},{6,22},{7,23},{8,24},{9,... | collective-permute-start | bytes 12582920 | tf_op jit(solution)/shard_map/ppermute | solution.py:267
  187.6 107.5 %collective-permute-start.32 = (bf16[2048,256]{1,0:T(8,128)(2,1)S(1)}, bf16[2048,256]{1,0:T(8,128)(2,1)S(1)}, u32[]{:S(2)}, u32[]{:S(2)}) collective-permute-start(bf16[2048,256]{1,0:T(8,128)(2,1)S(1)} %step.6.refs_4_.refs_2_), channel_id=1, source_target_pairs={{0,240},{1,241},{2,242},{3,243},{4,244},{5,245},{6,246},{7,247},{8... | collective-permute-start | bytes 3145736 | tf_op jit(solution)/shard_map/ppermute | solution.py:267
  203.8 8.9 %copy-start.7 = (bf16[256,2048]{1,0:T(8,128)(2,1)S(1)}, bf16[256,2048]{1,0:T(8,128)(2,1)}, u32[]{:S(2)}) copy-start(bf16[256,2048]{1,0:T(8,128)(2,1)} %copy-done.5) | copy-start | bytes 3145732
  203.9 91.2 %collective-permute-start.29 = (bf16[2048,256]{1,0:T(8,128)(2,1)S(1)}, bf16[2048,256]{1,0:T(8,128)(2,1)S(1)}, u32[]{:S(2)}, u32[]{:S(2)}) collective-permute-start(bf16[2048,256]{1,0:T(8,128)(2,1)S(1)} %step.9.refs_2_), channel_id=1, source_target_pairs={{0,240},{1,241},{2,242},{3,243},{4,244},{5,245},{6,246},{7,247},{8... | collective-permute-start | bytes 3145736 | tf_op jit(solution)/shard_map/ppermute | solution.py:267
  204.9 101.7 %collective-permute-start.33 = (bf16[2048,256]{1,0:T(8,128)(2,1)S(1)}, bf16[2048,256]{1,0:T(8,128)(2,1)S(1)}, u32[]{:S(2)}, u32[]{:S(2)}) collective-permute-start(bf16[2048,256]{1,0:T(8,128)(2,1)S(1)} %step.11.own), channel_id=1, source_target_pairs={{0,16},{1,17},{2,18},{3,19},{4,20},{5,21},{6,22},{7,23},{8,24},{9,... | collective-permute-start | bytes 3145736 | tf_op jit(solution)/shard_map/ppermute | solution.py:267
  212.6 94.0 %collective-permute-start.31 = (bf16[2048,256]{1,0:T(8,128)(2,1)S(1)}, bf16[2048,256]{1,0:T(8,128)(2,1)S(1)}, u32[]{:S(2)}, u32[]{:S(2)}) collective-permute-start(bf16[2048,256]{1,0:T(8,128)(2,1)S(1)} %step.11.own), channel_id=1, source_target_pairs={{0,16},{1,17},{2,18},{3,19},{4,20},{5,21},{6,22},{7,23},{8,24},{9,... | collective-permute-start | bytes 3145736 | tf_op jit(solution)/shard_map/ppermute | solution.py:267
  221.3 90.8 %collective-permute-start.30 = (bf16[2048,256]{1,0:T(8,128)(2,1)S(1)}, bf16[2048,256]{1,0:T(8,128)(2,1)S(1)}, u32[]{:S(2)}, u32[]{:S(2)}) collective-permute-start(bf16[2048,256]{1,0:T(8,128)(2,1)S(1)} %step.10.own), channel_id=1, source_target_pairs={{0,16},{1,17},{2,18},{3,19},{4,20},{5,21},{6,22},{7,23},{8,24},{9,... | collective-permute-start | bytes 3145736 | tf_op jit(solution)/shard_map/ppermute | solution.py:267
  295.1 17.1 %collective-permute-start.28 = (bf16[2048,256]{1,0:T(8,128)(2,1)S(1)}, bf16[2048,256]{1,0:T(8,128)(2,1)S(1)}, u32[]{:S(2)}, u32[]{:S(2)}) collective-permute-start(bf16[2048,256]{1,0:T(8,128)(2,1)S(1)} %step.10.own), channel_id=1, source_target_pairs={{0,16},{1,17},{2,18},{3,19},{4,20},{5,21},{6,22},{7,23},{8,24},{9,... | collective-permute-start | bytes 3145736 | tf_op jit(solution)/shard_map/ppermute | solution.py:267
  295.1 34.6 %collective-permute-start.26 = (bf16[2048,256]{1,0:T(8,128)(2,1)S(1)}, bf16[2048,256]{1,0:T(8,128)(2,1)S(1)}, u32[]{:S(2)}, u32[]{:S(2)}) collective-permute-start(bf16[2048,256]{1,0:T(8,128)(2,1)S(1)} %step.7.refs_2_), channel_id=1, source_target_pairs={{0,240},{1,241},{2,242},{3,243},{4,244},{5,245},{6,246},{7,247},{8... | collective-permute-start | bytes 3145736 | tf_op jit(solution)/shard_map/ppermute | solution.py:267
  306.6 26.4 %collective-permute-start.27 = (bf16[2048,256]{1,0:T(8,128)(2,1)S(1)}, bf16[2048,256]{1,0:T(8,128)(2,1)S(1)}, u32[]{:S(2)}, u32[]{:S(2)}) collective-permute-start(bf16[2048,256]{1,0:T(8,128)(2,1)S(1)} %step.8.own), channel_id=1, source_target_pairs={{0,16},{1,17},{2,18},{3,19},{4,20},{5,21},{6,22},{7,23},{8,24},{9,... | collective-permute-start | bytes 3145736 | tf_op jit(solution)/shard_map/ppermute | solution.py:267
  306.6 26.4 %collective-permute-start.25 = (bf16[2048,256]{1,0:T(8,128)(2,1)S(1)}, bf16[2048,256]{1,0:T(8,128)(2,1)S(1)}, u32[]{:S(2)}, u32[]{:S(2)}) collective-permute-start(bf16[2048,256]{1,0:T(8,128)(2,1)S(1)} %step.8.own), channel_id=1, source_target_pairs={{0,16},{1,17},{2,18},{3,19},{4,20},{5,21},{6,22},{7,23},{8,24},{9,... | collective-permute-start | bytes 3145736 | tf_op jit(solution)/shard_map/ppermute | solution.py:267

commit v4 on v3

--- a/solution.py
+++ b/solution.py
@@ -240,15 +240,20 @@
     width, both = own.shape
     uw = both // 2
     band = 512
-    read = pl.BlockSpec((band, both), lambda i: (i, 0))
-    write = pl.BlockSpec((band, uw), lambda i: (i, c))
+    read = pl.BlockSpec((band, both), lambda i, meta: (i, 0))
+    read_a = pl.BlockSpec((band, both), lambda i, meta: (i * meta[0], 0))
+    read_b = pl.BlockSpec((band, both), lambda i, meta: (i * (1 - meta[0]), 0))
+    write = pl.BlockSpec((band, uw), lambda i, meta: (i, c))
     extra = [] if done is None else list(done)
     return pl.pallas_call(
         mix_body,
-        grid=(width // band,),
+        grid_spec=pltpu.PrefetchScalarGridSpec(
+            num_scalar_prefetch=1,
+            grid=(width // band,),
+            in_specs=[read, read, read_a, read_b] + [ANY] * len(extra),
+            out_specs=(write, write),
+        ),
         out_shape=(jax.ShapeDtypeStruct((width, CHUNKS * uw), jnp.bfloat16),) * 2,
-        in_specs=[SMEM] + [read] * 4 + [ANY] * len(extra),
-        out_specs=(write, write),
         input_output_aliases={} if done is None else {5: 0, 6: 1},
         compiler_params=params(10),
         name="mix",

time: 336 us -> 336 us (level)
  no operation moved by 1% of the time
where the time goes in v4:
time: 336 us; the launch traced here: 335 us
  waiting for transfers between devices  214 us (64%)
  starting transfers between devices  72.3 us (22%)
  Pallas kernels  38 us (11%)
  local copies, waits for them, and re-layouts  9.55 us (3%)
    ppermute x34, waiting for transfers between devices, send(): return lax.ppermute(v, axes, device_pairs(groups, move))  214 us
    ppermute x34, starting transfers between devices, send(): return lax.ppermute(v, axes, device_pairs(groups, move))  64.6 us
    pallas_call x6, Pallas kernels, step_chunk(): pl.pallas_call(functools.partial(step_body, which, len(xs), c), grid=(1,)...  25.9 us
    unnamed x34, local copies, waits for them, and re-layouts  9.55 us
    all_to_all x1, starting transfers between devices, local(): hg = lax.all_to_all(hg, 'dp', split_axis=0, concat_axis=0, tiled=True)  7.75 us
    pallas_call x3, Pallas kernels, mix_chunk(): pl.pallas_call(mix_body, grid_spec=pltpu.PrefetchScalarGridSpec(num_scala...  7.23 us
  transfers between devices with their start and end apart: 35, of which 20 were waited for; matrix products, arithmetic and copies ran while one was open for 0% of the time, Pallas kernels for 10%

profile of v4, /device:TPU:2, one launch (start us, length us, event | category | flops | bytes accessed | tf_op | source)
XLA Modules:
  0.0 335.4 jit_solution(9911804473551694716)
XLA Ops:
  0.8 0.7 fusion
  1.5 1.3 collective-permute-done.got
  2.8 1.0 copy-done.8
  3.9 0.6 pick.1
  4.5 2.0 collective-permute-start.7
  6.5 2.1 collective-permute-start.6
  8.6 1.4 collective-permute-start.5
  10.1 5.8 %collective-permute-done.7.refs_4_ = bf16[64,2048]{1,0:T(8,128)(2,1)S(1)} collective-permute-done((bf16[64,2048]{1,0:T(8,128)(2,1)S(1)}, bf16[64,2048]{1,0:T(8,128)(2,1)S(1)}, u32[]{:S(2)}, u32[]{:S(2)}) %collective-permute-start.7) | collective-permute-done | bytes 262176 | tf_op jit(solution)/shard_map/ppermute | solution.py:272
  15.8 1.5 collective-permute-start.4
  17.3 1.7 collective-permute-start.10
  19.1 1.5 collective-permute-start.9
  20.6 2.3 collective-permute-done.5.refs_2_
  22.8 0.5 collective-permute-start.8
  23.3 2.0 collective-permute-done.11.refs_8_
  25.4 2.1 collective-permute-start.14
  27.5 1.4 collective-permute-start.13
  29.0 3.2 collective-permute-start.12
  32.1 2.0 collective-permute-done.9.refs_6_
  34.1 4.4 %collective-permute-done.8.refs_5_ = bf16[64,2048]{1,0:T(8,128)(2,1)S(1)} collective-permute-done((bf16[64,2048]{1,0:T(8,128)(2,1)S(1)}, bf16[64,2048]{1,0:T(8,128)(2,1)S(1)}, u32[]{:S(2)}, u32[]{:S(2)}) %collective-permute-start.8) | collective-permute-done | bytes 262176 | tf_op jit(solution)/shard_map/ppermute | solution.py:272
  38.5 1.2 collective-permute-done.14.refs_11_
  39.7 4.4 %collective-permute-done.13.refs_10_ = bf16[64,2048]{1,0:T(8,128)(2,1)S(1)} collective-permute-done((bf16[64,2048]{1,0:T(8,128)(2,1)S(1)}, bf16[64,2048]{1,0:T(8,128)(2,1)S(1)}, u32[]{:S(2)}, u32[]{:S(2)}) %collective-permute-start.13) | collective-permute-done | bytes 262176 | tf_op jit(solution)/shard_map/ppermute | solution.py:272
  44.2 2.0 collective-permute-done.12.refs_9_
  46.6 1.3 split.1
  47.9 7.7 %all-to-all-start = ((bf16[16,128,384]{2,1,0:T(8,128)(2,1)}), bf16[16,128,384]{2,1,0:T(8,128)(2,1)}, u32[]{:S(2)}, u32[]{:S(2)}) async-start(bf16[16,128,384]{2,1,0:T(8,128)(2,1)} %split.1), calls=%async_computation | async-start | bytes 3145728 | tf_op jit(solution)/shard_map/all_to_all | solution.py:308
  55.7 1.5 collective-permute-start.15
  57.2 33.8 %collective-permute-done.15.refs_0_ = bf16[64,2048]{1,0:T(8,128)(2,1)S(1)} collective-permute-done((bf16[64,2048]{1,0:T(8,128)(2,1)}, bf16[64,2048]{1,0:T(8,128)(2,1)S(1)}, u32[]{:S(2)}, u32[]{:S(2)}) %collective-permute-start.15) | collective-permute-done | bytes 262176 | tf_op jit(solution)/shard_map/ppermute | solution.py:272
  91.0 2.2 collective-permute-start.18
  93.2 1.5 collective-permute-start.17
  94.7 0.6 collective-permute-start.16
  95.2 6.8 %collective-permute-done.18.refs_3_ = bf16[64,2048]{1,0:T(8,128)(2,1)S(1)} collective-permute-done((bf16[64,2048]{1,0:T(8,128)(2,1)S(1)}, bf16[64,2048]{1,0:T(8,128)(2,1)S(1)}, u32[]{:S(2)}, u32[]{:S(2)}) %collective-permute-start.18) | collective-permute-done | bytes 262176 | tf_op jit(solution)/shard_map/ppermute | solution.py:272
  102.0 4.0 %collective-permute-done.17.refs_2_ = bf16[64,2048]{1,0:T(8,128)(2,1)S(1)} collective-permute-done((bf16[64,2048]{1,0:T(8,128)(2,1)S(1)}, bf16[64,2048]{1,0:T(8,128)(2,1)S(1)}, u32[]{:S(2)}, u32[]{:S(2)}) %collective-permute-start.17) | collective-permute-done | bytes 262176 | tf_op jit(solution)/shard_map/ppermute | solution.py:272
  106.3 5.9 %collective-permute-start.1 = (bf16[64,2048]{1,0:T(8,128)(2,1)S(1)}, bf16[64,2048]{1,0:T(8,128)(2,1)S(1)}, u32[]{:S(2)}, u32[]{:S(2)}) collective-permute-start(bf16[64,2048]{1,0:T(8,128)(2,1)S(1)} %get-tuple-element.10.refs_0_), channel_id=1, source_target_pairs={{0,4},{1,5},{2,6},{3,7},{4,8},{5,9},{6,10},{7,11},{8,12},{9,13},{1... | collective-permute-start | bytes 786440 | tf_op jit(solution)/shard_map/ppermute | solution.py:272
  112.2 6.1 %collective-permute-done.1.refs_1_ = bf16[64,2048]{1,0:T(8,128)(2,1)S(1)} collective-permute-done((bf16[64,2048]{1,0:T(8,128)(2,1)S(1)}, bf16[64,2048]{1,0:T(8,128)(2,1)S(1)}, u32[]{:S(2)}, u32[]{:S(2)}) %collective-permute-start.1) | collective-permute-done | bytes 262176 | tf_op jit(solution)/shard_map/ppermute | solution.py:272
  118.3 2.5 collective-permute-start.2
  120.8 1.4 copy-done.4
  122.2 1.2 pack.1.packed
  123.4 1.7 copy-done
  125.1 3.7 %collective-permute-done.2.refs_2_ = bf16[64,2048]{1,0:T(8,128)(2,1)} collective-permute-done((bf16[64,2048]{1,0:T(8,128)(2,1)S(1)}, bf16[64,2048]{1,0:T(8,128)(2,1)}, u32[]{:S(2)}, u32[]{:S(2)}) %collective-permute-start.2) | collective-permute-done | bytes 262176 | tf_op jit(solution)/shard_map/ppermute | solution.py:272
  128.8 1.0 copy-done.12
  129.8 1.9 copy-done.1
  131.7 1.2 copy-done.6
  132.9 1.2 copy-done.13
  134.2 7.9 %step.6.refs_4_.refs_2_ = bf16[2048,256]{1,0:T(8,128)(2,1)S(1)} custom-call(s32[17]{0:T(128)S(1)} %pad_add_fusion.meta, bf16[16,128,384]{2,1,0:T(8,128)(2,1)} %all-to-all-done.units, bf16[3,2048,256]{2,1,0:T(8,128)(2,1)S(1)} %copy-done.1, bf16[768,2048]{1,0:T(8,128)(2,1)S(1)} %cat.4.refs_0_, bf16[256,2048]{1,0:T(8,128)(2,1)S(1)} %copy-done.6, ...), custom_call_target="tpu_custom_call" | custom-call | flops 4294967296 | bytes 8388608 | tf_op jit(solution)/shard_map/step/pallas_call | solution.py:200
  142.1 1.1 cat.6.refs_0_
  143.2 2.1 collective-permute-start.23
  145.3 1.5 collective-permute-start.22
  146.8 0.6 collective-permute-start.21
  147.3 23.5 %collective-permute-done.23.refs_3_ = bf16[256,2048]{1,0:T(8,128)(2,1)S(1)} collective-permute-done((bf16[256,2048]{1,0:T(8,128)(2,1)S(1)}, bf16[256,2048]{1,0:T(8,128)(2,1)S(1)}, u32[]{:S(2)}, u32[]{:S(2)}) %collective-permute-start.23) | collective-permute-done | bytes 1048608 | tf_op jit(solution)/shard_map/ppermute | solution.py:272
  170.8 16.2 %collective-permute-done.22.refs_2_ = bf16[256,2048]{1,0:T(8,128)(2,1)S(1)} collective-permute-done((bf16[256,2048]{1,0:T(8,128)(2,1)S(1)}, bf16[256,2048]{1,0:T(8,128)(2,1)S(1)}, u32[]{:S(2)}, u32[]{:S(2)}) %collective-permute-start.22) | collective-permute-done | bytes 1048608 | tf_op jit(solution)/shard_map/ppermute | solution.py:272
  187.6 8.4 %collective-permute-start.32 = (bf16[2048,256]{1,0:T(8,128)(2,1)S(1)}, bf16[2048,256]{1,0:T(8,128)(2,1)S(1)}, u32[]{:S(2)}, u32[]{:S(2)}) collective-permute-start(bf16[2048,256]{1,0:T(8,128)(2,1)S(1)} %step.6.refs_4_.refs_2_), channel_id=1, source_target_pairs={{0,240},{1,241},{2,242},{3,243},{4,244},{5,245},{6,246},{7,247},{8... | collective-permute-start | bytes 3145736 | tf_op jit(solution)/shard_map/ppermute | solution.py:272
  196.0 7.9 %step.9.refs_2_ = bf16[2048,256]{1,0:T(8,128)(2,1)S(1)} custom-call(s32[17]{0:T(128)S(1)} %pad_add_fusion.meta, bf16[16,128,384]{2,1,0:T(8,128)(2,1)} %all-to-all-done.units, bf16[3,2048,256]{2,1,0:T(8,128)(2,1)S(1)} %copy-done.1, bf16[768,2048]{1,0:T(8,128)(2,1)S(1)} %cat.4.refs_0_, bf16[256,2048]{1,0:T(8,128)(2,1)S(1)} %copy-done.6, ...), custom_call_target="tpu_custom_call" | custom-call | flops 4294967296 | bytes 8388608 | tf_op jit(solution)/shard_map/step/pallas_call | solution.py:200
  204.0 0.9 step.11.own
  204.9 7.7 %collective-permute-start.33 = (bf16[2048,256]{1,0:T(8,128)(2,1)S(1)}, bf16[2048,256]{1,0:T(8,128)(2,1)S(1)}, u32[]{:S(2)}, u32[]{:S(2)}) collective-permute-start(bf16[2048,256]{1,0:T(8,128)(2,1)S(1)} %step.11.own), channel_id=1, source_target_pairs={{0,16},{1,17},{2,18},{3,19},{4,20},{5,21},{6,22},{7,23},{8,24},{9,... | collective-permute-start | bytes 3145736 | tf_op jit(solution)/shard_map/ppermute | solution.py:272
  212.7 7.9 %step.7.refs_2_ = bf16[2048,256]{1,0:T(8,128)(2,1)S(1)} custom-call(s32[17]{0:T(128)S(1)} %pad_add_fusion.meta, bf16[16,128,384]{2,1,0:T(8,128)(2,1)} %all-to-all-done.units, bf16[3,2048,256]{2,1,0:T(8,128)(2,1)S(1)} %copy-done.1, bf16[768,2048]{1,0:T(8,128)(2,1)S(1)} %cat.4.refs_0_, bf16[256,2048]{1,0:T(8,128)(2,1)S(1)} %copy-done.7, ...), custom_call_target="tpu_custom_call" | custom-call | flops 4294967296 | bytes 8388608 | tf_op jit(solution)/shard_map/step/pallas_call | solution.py:200
  220.6 0.7 step.10.own
  221.8 0.7 step.8.own
  222.4 72.6 %collective-permute-done.29.far_a = bf16[2048,256]{1,0:T(8,128)(2,1)S(1)} collective-permute-done((bf16[2048,256]{1,0:T(8,128)(2,1)S(1)}, bf16[2048,256]{1,0:T(8,128)(2,1)S(1)}, u32[]{:S(2)}, u32[]{:S(2)}) %collective-permute-start.29) | collective-permute-done | bytes 1048608 | tf_op jit(solution)/shard_map/ppermute | solution.py:272
  295.1 11.5 %collective-permute-start.26 = (bf16[2048,256]{1,0:T(8,128)(2,1)S(1)}, bf16[2048,256]{1,0:T(8,128)(2,1)S(1)}, u32[]{:S(2)}, u32[]{:S(2)}) collective-permute-start(bf16[2048,256]{1,0:T(8,128)(2,1)S(1)} %step.7.refs_2_), channel_id=1, source_target_pairs={{0,240},{1,241},{2,242},{3,243},{4,244},{5,245},{6,246},{7,247},{8... | collective-permute-start | bytes 3145736 | tf_op jit(solution)/shard_map/ppermute | solution.py:272
  306.7 2.4 mix.3
  309.1 3.0 collective-permute-done.30.far_b
  312.1 2.4 mix.4
  314.5 15.2 %collective-permute-done.26.far_a = bf16[2048,256]{1,0:T(8,128)(2,1)S(1)} collective-permute-done((bf16[2048,256]{1,0:T(8,128)(2,1)S(1)}, bf16[2048,256]{1,0:T(8,128)(2,1)S(1)}, u32[]{:S(2)}, u32[]{:S(2)}) %collective-permute-start.26) | collective-permute-done | bytes 1048608 | tf_op jit(solution)/shard_map/ppermute | solution.py:272
  329.7 3.3 collective-permute-done.27.far_b
  333.0 2.4 mix.5
  (60 shorter events, 2.2 us)
Async XLA Ops:
  0.6 2.2 collective-permute-start
  2.8 1.0 copy-start.8
  4.5 42.1 %copy-start.2 = (bf16[1,128,6144]{2,1,0:T(8,128)(2,1)S(1)}, bf16[1,128,6144]{2,1,0:T(8,128)(2,1)}, u32[]{:S(2)}) copy-start(bf16[1,128,6144]{2,1,0:T(8,128)(2,1)} %param.9) | copy-start | bytes 4718596
  4.5 11.3 %collective-permute-start.7 = (bf16[64,2048]{1,0:T(8,128)(2,1)S(1)}, bf16[64,2048]{1,0:T(8,128)(2,1)S(1)}, u32[]{:S(2)}, u32[]{:S(2)}) collective-permute-start(bf16[64,2048]{1,0:T(8,128)(2,1)S(1)} %get-tuple-element.11.refs_0_), channel_id=1, source_target_pairs={{0,4},{1,5},{2,6},{3,7},{4,8},{5,9},{6,10},{7,11},{8,12},{9,13},{1... | collective-permute-start | bytes 786440 | tf_op jit(solution)/shard_map/ppermute | solution.py:272
  6.5 12.5 %collective-permute-start.6 = (bf16[64,2048]{1,0:T(8,128)(2,1)S(1)}, bf16[64,2048]{1,0:T(8,128)(2,1)S(1)}, u32[]{:S(2)}, u32[]{:S(2)}) collective-permute-start(bf16[64,2048]{1,0:T(8,128)(2,1)S(1)} %get-tuple-element.11.refs_0_), channel_id=1, source_target_pairs={{0,2},{1,3},{2,0},{3,1},{4,6},{5,7},{6,4},{7,5},{8,10},{9,11},{10,... | collective-permute-start | bytes 786440 | tf_op jit(solution)/shard_map/ppermute | solution.py:272
  8.6 14.2 %collective-permute-start.5 = (bf16[64,2048]{1,0:T(8,128)(2,1)S(1)}, bf16[64,2048]{1,0:T(8,128)(2,1)S(1)}, u32[]{:S(2)}, u32[]{:S(2)}) collective-permute-start(bf16[64,2048]{1,0:T(8,128)(2,1)S(1)} %get-tuple-element.11.refs_0_), channel_id=1, source_target_pairs={{0,3},{1,0},{2,1},{3,2},{4,7},{5,4},{6,5},{7,6},{8,11},{9,8},{10,9... | collective-permute-start | bytes 786440 | tf_op jit(solution)/shard_map/ppermute | solution.py:272
  15.8 9.6 %collective-permute-start.11 = (bf16[64,2048]{1,0:T(8,128)(2,1)S(1)}, bf16[64,2048]{1,0:T(8,128)(2,1)S(1)}, u32[]{:S(2)}, u32[]{:S(2)}) collective-permute-start(bf16[64,2048]{1,0:T(8,128)(2,1)S(1)} %collective-permute-done.7.refs_4_), channel_id=1, source_target_pairs={{0,4},{1,5},{2,6},{3,7},{4,8},{5,9},{6,10},{7,11},{8,12},{9,13},{1... | collective-permute-start | bytes 786440 | tf_op jit(solution)/shard_map/ppermute | solution.py:272
  15.8 11.7 %collective-permute-start.4 = (bf16[64,2048]{1,0:T(8,128)(2,1)S(1)}, bf16[64,2048]{1,0:T(8,128)(2,1)S(1)}, u32[]{:S(2)}, u32[]{:S(2)}) collective-permute-start(bf16[64,2048]{1,0:T(8,128)(2,1)S(1)} %get-tuple-element.11.refs_0_), channel_id=1, source_target_pairs={{0,1},{1,2},{2,3},{3,0},{4,5},{5,6},{6,7},{7,4},{8,9},{9,10},{10,1... | collective-permute-start | bytes 786440 | tf_op jit(solution)/shard_map/ppermute | solution.py:272
  17.3 11.6 %collective-permute-start.10 = (bf16[64,2048]{1,0:T(8,128)(2,1)S(1)}, bf16[64,2048]{1,0:T(8,128)(2,1)S(1)}, u32[]{:S(2)}, u32[]{:S(2)}) collective-permute-start(bf16[64,2048]{1,0:T(8,128)(2,1)S(1)} %collective-permute-done.7.refs_4_), channel_id=1, source_target_pairs={{0,2},{1,3},{2,0},{3,1},{4,6},{5,7},{6,4},{7,5},{8,10},{9,11},{10,... | collective-permute-start | bytes 786440 | tf_op jit(solution)/shard_map/ppermute | solution.py:272
  19.1 15.0 %collective-permute-start.9 = (bf16[64,2048]{1,0:T(8,128)(2,1)S(1)}, bf16[64,2048]{1,0:T(8,128)(2,1)S(1)}, u32[]{:S(2)}, u32[]{:S(2)}) collective-permute-start(bf16[64,2048]{1,0:T(8,128)(2,1)S(1)} %collective-permute-done.7.refs_4_), channel_id=1, source_target_pairs={{0,3},{1,0},{2,1},{3,2},{4,7},{5,4},{6,5},{7,6},{8,11},{9,8},{10,9... | collective-permute-start | bytes 786440 | tf_op jit(solution)/shard_map/ppermute | solution.py:272
  22.8 15.7 %collective-permute-start.8 = (bf16[64,2048]{1,0:T(8,128)(2,1)S(1)}, bf16[64,2048]{1,0:T(8,128)(2,1)S(1)}, u32[]{:S(2)}, u32[]{:S(2)}) collective-permute-start(bf16[64,2048]{1,0:T(8,128)(2,1)S(1)} %collective-permute-done.7.refs_4_), channel_id=1, source_target_pairs={{0,1},{1,2},{2,3},{3,0},{4,5},{5,6},{6,7},{7,4},{8,9},{9,10},{10,1... | collective-permute-start | bytes 786440 | tf_op jit(solution)/shard_map/ppermute | solution.py:272
  25.4 21.1 %copy-start.9 = (bf16[64,2048]{1,0:T(8,128)(2,1)}, bf16[64,2048]{1,0:T(8,128)(2,1)S(1)}, u32[]{:S(2)}) copy-start(bf16[64,2048]{1,0:T(8,128)(2,1)S(1)} %collective-permute-done.11.refs_8_) | copy-start | bytes 786436
  25.4 14.3 %collective-permute-start.14 = (bf16[64,2048]{1,0:T(8,128)(2,1)S(1)}, bf16[64,2048]{1,0:T(8,128)(2,1)S(1)}, u32[]{:S(2)}, u32[]{:S(2)}) collective-permute-start(bf16[64,2048]{1,0:T(8,128)(2,1)S(1)} %collective-permute-done.11.refs_8_), channel_id=1, source_target_pairs={{0,2},{1,3},{2,0},{3,1},{4,6},{5,7},{6,4},{7,5},{8,10},{9,11},{10,... | collective-permute-start | bytes 786440 | tf_op jit(solution)/shard_map/ppermute | solution.py:272
  27.5 16.6 %collective-permute-start.13 = (bf16[64,2048]{1,0:T(8,128)(2,1)S(1)}, bf16[64,2048]{1,0:T(8,128)(2,1)S(1)}, u32[]{:S(2)}, u32[]{:S(2)}) collective-permute-start(bf16[64,2048]{1,0:T(8,128)(2,1)S(1)} %collective-permute-done.11.refs_8_), channel_id=1, source_target_pairs={{0,3},{1,0},{2,1},{3,2},{4,7},{5,4},{6,5},{7,6},{8,11},{9,8},{10,9... | collective-permute-start | bytes 786440 | tf_op jit(solution)/shard_map/ppermute | solution.py:272
  29.0 17.2 %collective-permute-start.12 = (bf16[64,2048]{1,0:T(8,128)(2,1)S(1)}, bf16[64,2048]{1,0:T(8,128)(2,1)S(1)}, u32[]{:S(2)}, u32[]{:S(2)}) collective-permute-start(bf16[64,2048]{1,0:T(8,128)(2,1)S(1)} %collective-permute-done.11.refs_8_), channel_id=1, source_target_pairs={{0,1},{1,2},{2,3},{3,0},{4,5},{5,6},{6,7},{7,4},{8,9},{9,10},{10,1... | collective-permute-start | bytes 786440 | tf_op jit(solution)/shard_map/ppermute | solution.py:272
  46.5 83.3 %collective-permute-start.19 = (bf16[768,2048]{1,0:T(8,128)(2,1)S(1)}, bf16[768,2048]{1,0:T(8,128)(2,1)}, u32[]{:S(2)}, u32[]{:S(2)}) collective-permute-start(bf16[768,2048]{1,0:T(8,128)(2,1)S(1)} %cat.4.refs_0_), channel_id=1, source_target_pairs={{0,16},{1,17},{2,18},{3,19},{4,20},{5,21},{6,22},{7,23},{8,24},{9,... | collective-permute-start | bytes 9437192 | tf_op jit(solution)/shard_map/ppermute | solution.py:272
  47.9 81.9 %all-to-all-start = ((bf16[16,128,384]{2,1,0:T(8,128)(2,1)}), bf16[16,128,384]{2,1,0:T(8,128)(2,1)}, u32[]{:S(2)}, u32[]{:S(2)}) async-start(bf16[16,128,384]{2,1,0:T(8,128)(2,1)} %split.1), calls=%async_computation | async-start | bytes 3145728 | tf_op jit(solution)/shard_map/all_to_all | solution.py:308
  55.7 65.2 %copy-start.3 = (bf16[1,2048,384]{2,1,0:T(8,128)(2,1)S(1)}, bf16[1,2048,384]{2,1,0:T(8,128)(2,1)}, u32[]{:S(2)}) copy-start(bf16[1,2048,384]{2,1,0:T(8,128)(2,1)} %param.10) | copy-start | bytes 4718596
  55.7 35.4 %collective-permute-start.15 = (bf16[64,2048]{1,0:T(8,128)(2,1)}, bf16[64,2048]{1,0:T(8,128)(2,1)S(1)}, u32[]{:S(2)}, u32[]{:S(2)}) collective-permute-start(bf16[64,2048]{1,0:T(8,128)(2,1)} %copy-done.9), channel_id=1, source_target_pairs={{0,4},{1,5},{2,6},{3,7},{4,8},{5,9},{6,10},{7,11},{8,12},{9,13},{1... | collective-permute-start | bytes 786440 | tf_op jit(solution)/shard_map/ppermute | solution.py:272
  91.0 11.0 %collective-permute-start.18 = (bf16[64,2048]{1,0:T(8,128)(2,1)S(1)}, bf16[64,2048]{1,0:T(8,128)(2,1)S(1)}, u32[]{:S(2)}, u32[]{:S(2)}) collective-permute-start(bf16[64,2048]{1,0:T(8,128)(2,1)S(1)} %collective-permute-done.15.refs_0_), channel_id=1, source_target_pairs={{0,2},{1,3},{2,0},{3,1},{4,6},{5,7},{6,4},{7,5},{8,10},{9,11},{10,... | collective-permute-start | bytes 786440 | tf_op jit(solution)/shard_map/ppermute | solution.py:272
  93.2 12.8 %collective-permute-start.17 = (bf16[64,2048]{1,0:T(8,128)(2,1)S(1)}, bf16[64,2048]{1,0:T(8,128)(2,1)S(1)}, u32[]{:S(2)}, u32[]{:S(2)}) collective-permute-start(bf16[64,2048]{1,0:T(8,128)(2,1)S(1)} %collective-permute-done.15.refs_0_), channel_id=1, source_target_pairs={{0,3},{1,0},{2,1},{3,2},{4,7},{5,4},{6,5},{7,6},{8,11},{9,8},{10,9... | collective-permute-start | bytes 786440 | tf_op jit(solution)/shard_map/ppermute | solution.py:272
  94.7 11.4 %collective-permute-start.16 = (bf16[64,2048]{1,0:T(8,128)(2,1)S(1)}, bf16[64,2048]{1,0:T(8,128)(2,1)S(1)}, u32[]{:S(2)}, u32[]{:S(2)}) collective-permute-start(bf16[64,2048]{1,0:T(8,128)(2,1)S(1)} %collective-permute-done.15.refs_0_), channel_id=1, source_target_pairs={{0,1},{1,2},{2,3},{3,0},{4,5},{5,6},{6,7},{7,4},{8,9},{9,10},{10,1... | collective-permute-start | bytes 786440 | tf_op jit(solution)/shard_map/ppermute | solution.py:272
  106.1 17.2 %copy-start.5 = (bf16[256,2048]{1,0:T(8,128)(2,1)}, bf16[256,2048]{1,0:T(8,128)(2,1)S(1)}, u32[]{:S(2)}) copy-start(bf16[256,2048]{1,0:T(8,128)(2,1)S(1)} %cat.5.refs_1_) | copy-start | bytes 3145732
  106.2 22.6 %collective-permute-start.20 = (bf16[256,2048]{1,0:T(8,128)(2,1)S(1)}, bf16[256,2048]{1,0:T(8,128)(2,1)S(1)}, u32[]{:S(2)}, u32[]{:S(2)}) collective-permute-start(bf16[256,2048]{1,0:T(8,128)(2,1)S(1)} %cat.5.refs_1_), channel_id=1, source_target_pairs={{0,16},{1,17},{2,18},{3,19},{4,20},{5,21},{6,22},{7,23},{8,24},{9,... | collective-permute-start | bytes 3145736 | tf_op jit(solution)/shard_map/ppermute | solution.py:272
  106.3 12.1 %collective-permute-start.1 = (bf16[64,2048]{1,0:T(8,128)(2,1)S(1)}, bf16[64,2048]{1,0:T(8,128)(2,1)S(1)}, u32[]{:S(2)}, u32[]{:S(2)}) collective-permute-start(bf16[64,2048]{1,0:T(8,128)(2,1)S(1)} %get-tuple-element.10.refs_0_), channel_id=1, source_target_pairs={{0,4},{1,5},{2,6},{3,7},{4,8},{5,9},{6,10},{7,11},{8,12},{9,13},{1... | collective-permute-start | bytes 786440 | tf_op jit(solution)/shard_map/ppermute | solution.py:272
  118.3 5.1 %copy-start.10 = (bf16[64,2048]{1,0:T(8,128)(2,1)}, bf16[64,2048]{1,0:T(8,128)(2,1)S(1)}, u32[]{:S(2)}) copy-start(bf16[64,2048]{1,0:T(8,128)(2,1)S(1)} %collective-permute-done.1.refs_1_) | copy-start | bytes 786436
  118.3 10.4 %collective-permute-start.2 = (bf16[64,2048]{1,0:T(8,128)(2,1)S(1)}, bf16[64,2048]{1,0:T(8,128)(2,1)}, u32[]{:S(2)}, u32[]{:S(2)}) collective-permute-start(bf16[64,2048]{1,0:T(8,128)(2,1)S(1)} %collective-permute-done.1.refs_1_), channel_id=1, source_target_pairs={{0,4},{1,5},{2,6},{3,7},{4,8},{5,9},{6,10},{7,11},{8,12},{9,13},{1... | collective-permute-start | bytes 786440 | tf_op jit(solution)/shard_map/ppermute | solution.py:272
  120.8 1.4 copy-start.4
  123.4 1.7 copy-start
  128.8 13.3 %collective-permute-start.3 = (bf16[64,2048]{1,0:T(8,128)(2,1)}, bf16[64,2048]{1,0:T(8,128)(2,1)}, u32[]{:S(2)}, u32[]{:S(2)}) collective-permute-start(bf16[64,2048]{1,0:T(8,128)(2,1)} %collective-permute-done.2.refs_2_), channel_id=1, source_target_pairs={{0,4},{1,5},{2,6},{3,7},{4,8},{5,9},{6,10},{7,11},{8,12},{9,13},{1... | collective-permute-start | bytes 786440 | tf_op jit(solution)/shard_map/ppermute | solution.py:272
  128.8 1.0 copy-start.12
  129.8 1.9 copy-start.1
  131.7 1.2 copy-start.6
  132.9 1.2 copy-start.13
  134.2 7.9 %copy-start.11 = (bf16[64,2048]{1,0:T(8,128)(2,1)S(1)}, bf16[64,2048]{1,0:T(8,128)(2,1)}, u32[]{:S(2)}) copy-start(bf16[64,2048]{1,0:T(8,128)(2,1)} %copy-done.10) | copy-start | bytes 786436
  143.2 44.3 %copy-start.15 = (s32[16]{0:T(128)S(1)}, s32[16]{0:T(128)}, u32[]{:S(2)}) copy-start(s32[16]{0:T(128)} %constant.84) | copy-start | bytes 196
  143.2 44.3 %copy-start.16 = (s32[16]{0:T(128)S(1)}, s32[16]{0:T(128)}, u32[]{:S(2)}) copy-start(s32[16]{0:T(128)} %constant.83) | copy-start | bytes 196
  143.2 52.8 %copy-start.14 = (bf16[256,2048]{1,0:T(8,128)(2,1)S(1)}, bf16[256,2048]{1,0:T(8,128)(2,1)}, u32[]{:S(2)}) copy-start(bf16[256,2048]{1,0:T(8,128)(2,1)} %copy-done.12) | copy-start | bytes 3145732
  143.2 27.6 %collective-permute-start.23 = (bf16[256,2048]{1,0:T(8,128)(2,1)S(1)}, bf16[256,2048]{1,0:T(8,128)(2,1)S(1)}, u32[]{:S(2)}, u32[]{:S(2)}) collective-permute-start(bf16[256,2048]{1,0:T(8,128)(2,1)S(1)} %cat.6.refs_0_), channel_id=1, source_target_pairs={{0,2},{1,3},{2,0},{3,1},{4,6},{5,7},{6,4},{7,5},{8,10},{9,11},{10,... | collective-permute-start | bytes 3145736 | tf_op jit(solution)/shard_map/ppermute | solution.py:272
  145.3 41.7 %collective-permute-start.22 = (bf16[256,2048]{1,0:T(8,128)(2,1)S(1)}, bf16[256,2048]{1,0:T(8,128)(2,1)S(1)}, u32[]{:S(2)}, u32[]{:S(2)}) collective-permute-start(bf16[256,2048]{1,0:T(8,128)(2,1)S(1)} %cat.6.refs_0_), channel_id=1, source_target_pairs={{0,3},{1,0},{2,1},{3,2},{4,7},{5,4},{6,5},{7,6},{8,11},{9,8},{10,9... | collective-permute-start | bytes 3145736 | tf_op jit(solution)/shard_map/ppermute | solution.py:272
  146.8 40.3 %collective-permute-start.21 = (bf16[256,2048]{1,0:T(8,128)(2,1)S(1)}, bf16[256,2048]{1,0:T(8,128)(2,1)S(1)}, u32[]{:S(2)}, u32[]{:S(2)}) collective-permute-start(bf16[256,2048]{1,0:T(8,128)(2,1)S(1)} %cat.6.refs_0_), channel_id=1, source_target_pairs={{0,1},{1,2},{2,3},{3,0},{4,5},{5,6},{6,7},{7,4},{8,9},{9,10},{10,1... | collective-permute-start | bytes 3145736 | tf_op jit(solution)/shard_map/ppermute | solution.py:272
  187.4 16.6 %collective-permute-start.24 = (bf16[1024,2048]{1,0:T(8,128)(2,1)S(1)}, bf16[1024,2048]{1,0:T(8,128)(2,1)S(1)}, u32[]{:S(2)}, u32[]{:S(2)}) collective-permute-start(bf16[1024,2048]{1,0:T(8,128)(2,1)S(1)} %cat.7.refs_0_), channel_id=1, source_target_pairs={{0,16},{1,17},{2,18},{3,19},{4,20},{5,21},{6,22},{7,23},{8,24},{9,... | collective-permute-start | bytes 12582920 | tf_op jit(solution)/shard_map/ppermute | solution.py:272
  187.6 107.5 %collective-permute-start.32 = (bf16[2048,256]{1,0:T(8,128)(2,1)S(1)}, bf16[2048,256]{1,0:T(8,128)(2,1)S(1)}, u32[]{:S(2)}, u32[]{:S(2)}) collective-permute-start(bf16[2048,256]{1,0:T(8,128)(2,1)S(1)} %step.6.refs_4_.refs_2_), channel_id=1, source_target_pairs={{0,240},{1,241},{2,242},{3,243},{4,244},{5,245},{6,246},{7,247},{8... | collective-permute-start | bytes 3145736 | tf_op jit(solution)/shard_map/ppermute | solution.py:272
  203.8 8.9 %copy-start.7 = (bf16[256,2048]{1,0:T(8,128)(2,1)S(1)}, bf16[256,2048]{1,0:T(8,128)(2,1)}, u32[]{:S(2)}) copy-start(bf16[256,2048]{1,0:T(8,128)(2,1)} %copy-done.5) | copy-start | bytes 3145732
  203.9 91.2 %collective-permute-start.29 = (bf16[2048,256]{1,0:T(8,128)(2,1)S(1)}, bf16[2048,256]{1,0:T(8,128)(2,1)S(1)}, u32[]{:S(2)}, u32[]{:S(2)}) collective-permute-start(bf16[2048,256]{1,0:T(8,128)(2,1)S(1)} %step.9.refs_2_), channel_id=1, source_target_pairs={{0,240},{1,241},{2,242},{3,243},{4,244},{5,245},{6,246},{7,247},{8... | collective-permute-start | bytes 3145736 | tf_op jit(solution)/shard_map/ppermute | solution.py:272
  204.9 101.7 %collective-permute-start.33 = (bf16[2048,256]{1,0:T(8,128)(2,1)S(1)}, bf16[2048,256]{1,0:T(8,128)(2,1)S(1)}, u32[]{:S(2)}, u32[]{:S(2)}) collective-permute-start(bf16[2048,256]{1,0:T(8,128)(2,1)S(1)} %step.11.own), channel_id=1, source_target_pairs={{0,16},{1,17},{2,18},{3,19},{4,20},{5,21},{6,22},{7,23},{8,24},{9,... | collective-permute-start | bytes 3145736 | tf_op jit(solution)/shard_map/ppermute | solution.py:272
  212.6 94.0 %collective-permute-start.31 = (bf16[2048,256]{1,0:T(8,128)(2,1)S(1)}, bf16[2048,256]{1,0:T(8,128)(2,1)S(1)}, u32[]{:S(2)}, u32[]{:S(2)}) collective-permute-start(bf16[2048,256]{1,0:T(8,128)(2,1)S(1)} %step.11.own), channel_id=1, source_target_pairs={{0,16},{1,17},{2,18},{3,19},{4,20},{5,21},{6,22},{7,23},{8,24},{9,... | collective-permute-start | bytes 3145736 | tf_op jit(solution)/shard_map/ppermute | solution.py:272
  221.3 90.8 %collective-permute-start.30 = (bf16[2048,256]{1,0:T(8,128)(2,1)S(1)}, bf16[2048,256]{1,0:T(8,128)(2,1)S(1)}, u32[]{:S(2)}, u32[]{:S(2)}) collective-permute-start(bf16[2048,256]{1,0:T(8,128)(2,1)S(1)} %step.10.own), channel_id=1, source_target_pairs={{0,16},{1,17},{2,18},{3,19},{4,20},{5,21},{6,22},{7,23},{8,24},{9,... | collective-permute-start | bytes 3145736 | tf_op jit(solution)/shard_map/ppermute | solution.py:272
  295.1 17.1 %collective-permute-start.28 = (bf16[2048,256]{1,0:T(8,128)(2,1)S(1)}, bf16[2048,256]{1,0:T(8,128)(2,1)S(1)}, u32[]{:S(2)}, u32[]{:S(2)}) collective-permute-start(bf16[2048,256]{1,0:T(8,128)(2,1)S(1)} %step.10.own), channel_id=1, source_target_pairs={{0,16},{1,17},{2,18},{3,19},{4,20},{5,21},{6,22},{7,23},{8,24},{9,... | collective-permute-start | bytes 3145736 | tf_op jit(solution)/shard_map/ppermute | solution.py:272
  295.1 34.6 %collective-permute-start.26 = (bf16[2048,256]{1,0:T(8,128)(2,1)S(1)}, bf16[2048,256]{1,0:T(8,128)(2,1)S(1)}, u32[]{:S(2)}, u32[]{:S(2)}) collective-permute-start(bf16[2048,256]{1,0:T(8,128)(2,1)S(1)} %step.7.refs_2_), channel_id=1, source_target_pairs={{0,240},{1,241},{2,242},{3,243},{4,244},{5,245},{6,246},{7,247},{8... | collective-permute-start | bytes 3145736 | tf_op jit(solution)/shard_map/ppermute | solution.py:272
  306.6 26.4 %collective-permute-start.27 = (bf16[2048,256]{1,0:T(8,128)(2,1)S(1)}, bf16[2048,256]{1,0:T(8,128)(2,1)S(1)}, u32[]{:S(2)}, u32[]{:S(2)}) collective-permute-start(bf16[2048,256]{1,0:T(8,128)(2,1)S(1)} %step.8.own), channel_id=1, source_target_pairs={{0,16},{1,17},{2,18},{3,19},{4,20},{5,21},{6,22},{7,23},{8,24},{9,... | collective-permute-start | bytes 3145736 | tf_op jit(solution)/shard_map/ppermute | solution.py:272
  306.6 26.4 %collective-permute-start.25 = (bf16[2048,256]{1,0:T(8,128)(2,1)S(1)}, bf16[2048,256]{1,0:T(8,128)(2,1)S(1)}, u32[]{:S(2)}, u32[]{:S(2)}) collective-permute-start(bf16[2048,256]{1,0:T(8,128)(2,1)S(1)} %step.8.own), channel_id=1, source_target_pairs={{0,16},{1,17},{2,18},{3,19},{4,20},{5,21},{6,22},{7,23},{8,24},{9,... | collective-permute-start | bytes 3145736 | tf_op jit(solution)/shard_map/ppermute | solution.py:272
